TPU v7x, 32 devices: a whole 2x2x4 slice. The times are simulated.
32 devices in a mesh: tm: 16 (over z, x, core), freq: 2 (over y).
Axes of the slice: x: 2, y: 2, z: 4, core: 2. Of those that a mesh axis runs over, the one named last changes fastest.
Arguments:
- strengths: bfloat16 [2, 8, 256, 32768], P(None, 'freq', None, 'tm'), may hold values from -6 to 6
- sample_cell: int32 [32768], P('tm'), may hold values from 0 to 16383, as said below
- sample_frac: float32 [32768], P('tm'), may hold values from 0 to 1
Outputs:
- spectra: float32 [2, 8, 256, 4, 32, 128], P(None, None, 'tm', 'freq')
Inputs may be any that keep to these rules, and one draw needn't show every extreme that they name: `sample_cell`: the samples of the i-th aligned block of 2048 samples lie in cells i * 1024 to (i + 1) * 1024 - 1; in every block the first sample lies in the first of these cells and the second sample in the last.
All inputs are finite; a program needn't handle non-finite values.
Results may differ from a plain program's by a relative error of at most 0.0037.
Values may be sent and summed in bfloat16 or wider, within the bound.
A program may use at most 128 MiB of HBM per device.

v0:
```python
import functools
import math

import jax
import jax.numpy as jnp
import numpy as np
from jax import lax
from jax.experimental import pallas as pl
from jax.experimental.pallas import tpu as pltpu
from jax.sharding import PartitionSpec as P

TAPS = 8
HALF = TAPS // 2
GRID_DEV = 1024
FFT_LO = 32
FFT_HI = 128
FFTLEN = 4096
SHARP = 0.3
MESH = pl.DeviceIdType.MESH
SLABS = GRID_DEV // FFT_HI
PER_FRAME = FFTLEN // GRID_DEV


def tap_table(local_cell, fraction, columns):
    offset = columns[None, :] - local_cell[:, None] - 1
    inside = (offset >= 0) & (offset < TAPS)
    shifted = offset.astype(jnp.float32) - float(HALF - 1) - fraction[:, None]
    values = jnp.exp(-SHARP * (shifted * shifted))
    return jnp.where(inside, values, 0.0).astype(jnp.bfloat16)


def exchange_kernel(
    n_tm, n_fq, strengths, halo, table, select, out, held, src, load, send1, recv1, send2, recv2, local_sem
):
    t = lax.axis_index("tm")
    f = lax.axis_index("freq")
    span = n_tm // n_fq
    slot = lax.rem(t, span)
    home = lax.div(t, span)
    barrier = pltpu.get_barrier_semaphore()

    def greet_tm(i, c):
        pl.semaphore_signal(barrier, inc=1, device_id=(lax.rem(t + i, n_tm), f), device_id_type=MESH)
        return c

    def greet_fq(i, c):
        pl.semaphore_signal(barrier, inc=1, device_id=(t, lax.rem(f + i, n_fq)), device_id_type=MESH)
        return c

    lax.fori_loop(1, n_tm, greet_tm, 0)
    lax.fori_loop(1, n_fq, greet_fq, 0)
    half = n_tm // 2
    upper = lax.div(t, half)
    chunk = held.shape[3]
    rows = src.shape[2]

    def dest(i):
        side = jnp.where(i < half, 1 - upper, upper)
        return side * half + lax.rem(t + 1 + i, half)

    def fetch(i):
        channels = pl.ds(pl.multiple_of(dest(i) * chunk, chunk), chunk)
        return pltpu.make_async_copy(strengths.at[:, :, channels, :], held.at[i], load.at[i])

    def fetch_one(i, c):
        fetch(i).start()
        return c

    lax.fori_loop(0, n_tm, fetch_one, 0)

    def make(i):
        fetch(i).wait()
        channels = pl.ds(pl.multiple_of(dest(i) * chunk, chunk), chunk)
        x = held[i].reshape(rows, held.shape[4])
        h = halo[:, :, channels, :].reshape(rows, halo.shape[3])
        acc = jnp.dot(x, table[...], preferred_element_type=jnp.float32)
        acc = acc + jnp.dot(h, select[...], preferred_element_type=jnp.float32)
        acc = acc.astype(jnp.bfloat16)
        for j in range(SLABS):
            src[dest(i), j] = acc[:, j * FFT_HI : (j + 1) * FFT_HI]

    make(0)
    pl.semaphore_wait(barrier, n_tm - 1 + n_fq - 1)

    def place(target):
        return jnp.where(target == f, f, n_fq + target)

    def first(peer):
        return pltpu.make_async_remote_copy(
            src_ref=src.at[peer],
            dst_ref=out.at[place(home), slot],
            send_sem=send1.at[peer],
            recv_sem=recv1.at[t],
            device_id=(peer, f),
            device_id_type=MESH,
        )

    def first_landed(origin):
        return pltpu.make_async_remote_copy(
            src_ref=src.at[origin],
            dst_ref=out.at[place(lax.div(origin, span)), lax.rem(origin, span)],
            send_sem=send1.at[origin],
            recv_sem=recv1.at[origin],
            device_id=(origin, f),
            device_id_type=MESH,
        )

    def second(target, s):
        return pltpu.make_async_remote_copy(
            src_ref=out.at[n_fq + target, s],
            dst_ref=out.at[f, s],
            send_sem=send2.at[target, s],
            recv_sem=recv2.at[f, s],
            device_id=(t, target),
            device_id_type=MESH,
        )

    def second_landed(origin, s):
        return pltpu.make_async_remote_copy(
            src_ref=out.at[n_fq + origin, s],
            dst_ref=out.at[origin, s],
            send_sem=send2.at[origin, s],
            recv_sem=recv2.at[origin, s],
            device_id=(t, origin),
            device_id_type=MESH,
        )

    def step(i, c):
        make(i)
        first(dest(i - 1)).start()
        return c

    lax.fori_loop(1, n_tm, step, 0)
    own = pltpu.make_async_copy(src.at[t], out.at[place(home), slot], local_sem)
    own.start()
    own.wait()

    def relay_group(k, c):
        target = lax.rem(f + k, n_fq)

        def relay(i, c):
            s = lax.rem(slot + 2 * span - 1 - i, span)
            origin = target * span + s

            @pl.when(origin != t)
            def _():
                first_landed(origin).wait_recv()

            second(target, s).start()
            return c

        return lax.fori_loop(0, span, relay, c)

    lax.fori_loop(1, n_fq, relay_group, 0)

    def kept(s, c):
        origin = f * span + s

        @pl.when(origin != t)
        def _():
            first_landed(origin).wait_recv()

        return c

    lax.fori_loop(0, span, kept, 0)

    def finish_first(i, c):
        first(lax.rem(t + i, n_tm)).wait_send()
        return c

    lax.fori_loop(1, n_tm, finish_first, 0)

    def finish_group(k, c):
        other = lax.rem(f + k, n_fq)

        def finish(s, c):
            second(other, s).wait_send()
            second_landed(other, s).wait_recv()
            return c

        return lax.fori_loop(0, span, finish, c)

    lax.fori_loop(1, n_fq, finish_group, 0)


def exchange(strengths, halo_cols, table, select, n_tm, n_fq):
    parts, groups, channels, samples = strengths.shape
    span = n_tm // n_fq
    chunk = channels // n_tm
    block = (SLABS, parts * groups * chunk, FFT_HI)
    return pl.pallas_call(
        functools.partial(exchange_kernel, n_tm, n_fq),
        out_shape=jax.ShapeDtypeStruct((2 * n_fq, span) + block, jnp.bfloat16),
        in_specs=[pl.BlockSpec(memory_space=pl.ANY)] + [pl.BlockSpec(memory_space=pltpu.VMEM)] * 3,
        out_specs=pl.BlockSpec(memory_space=pl.ANY),
        scratch_shapes=[
            pltpu.VMEM((n_tm, parts, groups, chunk, samples), jnp.bfloat16),
            pltpu.VMEM((n_tm,) + block, jnp.bfloat16),
            pltpu.SemaphoreType.DMA((n_tm,)),
            pltpu.SemaphoreType.DMA((n_tm,)),
            pltpu.SemaphoreType.DMA((n_tm,)),
            pltpu.SemaphoreType.DMA((n_fq, span)),
            pltpu.SemaphoreType.DMA((n_fq, span)),
            pltpu.SemaphoreType.DMA,
        ],
        compiler_params=pltpu.CompilerParams(
            collective_id=0, has_side_effects=True, vmem_limit_bytes=48 * 1024 * 1024
        ),
        name="spread_exchange",
    )(strengths, halo_cols, table, select)


def fft_list(re, im):
    n = len(re)
    if n == 1:
        return re, im
    er, ei = fft_list(re[0::2], im[0::2])
    orr, oi = fft_list(re[1::2], im[1::2])
    out_r, out_i = [None] * n, [None] * n
    for k in range(n // 2):
        c, s = math.cos(2 * math.pi * k / n), math.sin(2 * math.pi * k / n)
        a, b = orr[k], oi[k]
        if k == 0:
            tr, ti = a, b
        elif 4 * k == n:
            tr, ti = b, -a
        elif 8 * k == n:
            tr, ti = (a + b) * c, (b - a) * c
        elif 8 * k == 3 * n:
            tr, ti = (b - a) * s, -(a + b) * s
        else:
            tr, ti = a * c + b * s, b * c - a * s
        out_r[k], out_i[k] = er[k] + tr, ei[k] + ti
        out_r[k + n // 2], out_i[k + n // 2] = er[k] - tr, ei[k] - ti
    return out_r, out_i


def transform_kernel(x_ref, tc_ref, ts_ref, hi_ref, o_ref, lhs):
    chunk = x_ref.shape[5]
    re = [x_ref[0, n // SLABS, n % SLABS, 0, 0].astype(jnp.float32) for n in range(FFT_LO)]
    im = [x_ref[0, n // SLABS, n % SLABS, 1, 0].astype(jnp.float32) for n in range(FFT_LO)]
    re, im = fft_list(re, im)
    for a in range(FFT_LO):
        c = tc_ref[a : a + 1, :]
        s = ts_ref[a : a + 1, :]
        rows = pl.ds(a * chunk, chunk)
        lhs[rows, :FFT_HI] = (re[a] * c + im[a] * s).astype(jnp.bfloat16)
        lhs[rows, FFT_HI:] = (im[a] * c - re[a] * s).astype(jnp.bfloat16)
    x = lhs[...]
    y = jnp.dot(x, hi_ref[...], preferred_element_type=jnp.float32)
    flat = o_ref.reshape(2, chunk * FFT_LO, FFT_HI)
    for a in range(FFT_LO):
        for p in range(2):
            flat[p, pl.ds(a, chunk, stride=FFT_LO), :] = y[
                a * chunk : (a + 1) * chunk, p * FFT_HI : (p + 1) * FFT_HI
            ]


def transform(held, n_fq, groups, chunk, frames):
    span = held.shape[1]
    x = held.reshape(2 * n_fq, span, SLABS, 2, groups, chunk, FFT_HI)
    low = np.arange(FFT_LO)[:, None] * np.arange(FFT_HI)[None, :] * (2 * math.pi / FFTLEN)
    high = np.arange(FFT_HI)[:, None] * np.arange(FFT_HI)[None, :] % FFT_HI * (2 * math.pi / FFT_HI)
    hc, hs = np.cos(high), np.sin(high)
    full = np.block([[hc, -hs], [hs, hc]]).astype(np.float32) / math.sqrt(FFTLEN)
    hi = full.astype(jnp.bfloat16)
    whole = lambda shape: pl.BlockSpec(shape, lambda f, g, m: (0, 0))
    return pl.pallas_call(
        transform_kernel,
        out_shape=jax.ShapeDtypeStruct(
            (2, n_fq * groups, chunk, frames, FFT_LO, FFT_HI), jnp.float32
        ),
        grid=(n_fq, groups, frames),
        in_specs=[
            pl.BlockSpec(
                (1, PER_FRAME, SLABS, 2, 1, chunk, FFT_HI), lambda f, g, m: (f, m, 0, 0, g, 0, 0)
            ),
            whole((FFT_LO, FFT_HI)),
            whole((FFT_LO, FFT_HI)),
            whole((2 * FFT_HI, 2 * FFT_HI)),
        ],
        out_specs=pl.BlockSpec(
            (2, 1, chunk, 1, FFT_LO, FFT_HI), lambda f, g, m: (0, f * groups + g, 0, m, 0, 0)
        ),
        scratch_shapes=[
            pltpu.VMEM((FFT_LO * chunk, 2 * FFT_HI), jnp.bfloat16),
        ],
        name="transform",
    )(
        x,
        jnp.asarray(np.cos(low), jnp.float32),
        jnp.asarray(np.sin(low), jnp.float32),
        jnp.asarray(hi),
    )


def shards(strengths, sample_cell, sample_frac):
    n_tm, n_fq = lax.axis_size("tm"), lax.axis_size("freq")
    parts, groups, channels, samples = strengths.shape
    local_cell = sample_cell - lax.axis_index("tm") * GRID_DEV
    edge_columns = jnp.concatenate(
        [
            jnp.arange(HALF, dtype=jnp.int32),
            jnp.arange(GRID_DEV + HALF, GRID_DEV + TAPS, dtype=jnp.int32),
        ]
    )
    edge_table = tap_table(local_cell, sample_frac, edge_columns)
    edges = lax.dot_general(
        edge_table,
        strengths.reshape(parts * groups * channels, samples),
        (((0,), (1,)), ((), ())),
        preferred_element_type=jnp.float32,
    )
    from_left = lax.ppermute(edges[HALF:], "tm", [(i, (i + 1) % n_tm) for i in range(n_tm)])
    from_right = lax.ppermute(edges[:HALF], "tm", [((i + 1) % n_tm, i) for i in range(n_tm)])
    table = tap_table(local_cell, sample_frac, jnp.arange(HALF, HALF + GRID_DEV, dtype=jnp.int32))
    halo = jnp.concatenate([from_left, from_right], axis=0)
    h0 = lax.reduce_precision(halo, 8, 7)
    h1 = lax.reduce_precision(halo - h0, 8, 7)
    h2 = halo - h0 - h1
    split = jnp.concatenate([h0, h1, h2], axis=0)
    halo_cols = jnp.pad(split.T, ((0, 0), (0, 128 - 3 * TAPS))).astype(jnp.bfloat16)
    pick = np.zeros((128, GRID_DEV), np.float32)
    for r in range(3):
        for k in range(HALF):
            pick[r * TAPS + k, k] = 1.0
            pick[r * TAPS + HALF + k, GRID_DEV - HALF + k] = 1.0
    held = exchange(
        strengths,
        halo_cols.reshape(parts, groups, channels, 128),
        table,
        jnp.asarray(pick, jnp.bfloat16),
        n_tm,
        n_fq,
    )
    frames = n_tm // PER_FRAME // n_fq
    return transform(held, n_fq, groups, channels // n_tm, frames)


def solution(mesh):
    placed = (P(None, "freq", None, "tm"), P("tm"), P("tm"))
    return jax.shard_map(
        shards,
        mesh=mesh,
        in_specs=placed,
        out_specs=P(None, None, "tm", "freq", None, None),
        check_vma=False,
    )
```

profile of v0, /device:TPU:5, one launch (start us, length us, event | category | flops | bytes accessed | tf_op | source)
XLA Modules:
  0.0 144.0 jit_solution(16430014768831490943)
XLA Ops:
  0.0 0.0 copy-start.1
  0.0 0.0 copy-start.2
  0.0 0.1 pad_add_fusion
  0.1 0.7 broadcast_subtract_fusion
  0.8 5.7 %fusion.7 = f32[8,2048]{1,0:T(8,128)S(1)} fusion(bf16[2048,2048]{1,0:T(8,128)(2,1)} %bitcast.7, f32[2048]{0:T(1024)} %param.9, s32[2048]{0:T(1024)S(1)} %broadcast_subtract_fusion, s32[8]{0:T(128)S(1)} %pad_add_fusion), kind=kOutput, calls=%fused_computation.17 | convolution fusion | flops 67305472 | bytes 8470560 | tf_op jit(solution)/shard_map/dot_general | solution.py:308
  6.5 1.8 %collective-permute-start = (f32[4,2048]{1,0:T(4,128)S(1)}, f32[4,2048]{1,0:T(4,128)S(1)}, u32[]{:S(2)}, u32[]{:S(2)}) collective-permute-start(f32[4,2048]{1,0:T(4,128)S(1)} %get-tuple-element.8), channel_id=1, source_target_pairs={{0,2},{2,4},{4,6},{6,8},{8,10},{10,12},{12,14},{14,16},{16,18},{18... | collective-permute-start | bytes 98312 | tf_op jit(solution)/shard_map/ppermute | solution.py:314
  8.3 0.0 collective-permute-start.1
  8.3 0.0 copy-done.2
  8.3 6.2 %select_convert_fusion.table = bf16[2048,1024]{1,0:T(8,128)(2,1)} fusion(f32[2048]{0:T(1024)S(1)} %copy-done.2, s32[2048]{0:T(1024)S(1)} %broadcast_subtract_fusion, s32[1024]{0:T(1024)S(1)} %iota_add_fusion), kind=kLoop, calls=%fused_computation | loop fusion | flops 25165824 | bytes 4214784 | tf_op jit(solution)/shard_map/convert_element_type | solution.py:29
  14.5 0.0 collective-permute-done
  14.5 0.0 collective-permute-done.1
  14.6 0.3 copy.10
  14.8 0.1 pad.5.clone
  14.9 0.0 copy-done.1
  15.0 0.0 copy-start
  15.0 2.2 %copy-done = bf16[2048,1024]{1,0:T(8,128)(2,1)S(1)} copy-done((bf16[2048,1024]{1,0:T(8,128)(2,1)S(1)}, bf16[2048,1024]{1,0:T(8,128)(2,1)}, u32[]{:S(2)}) %copy-start) | copy-done | bytes 4194328
  17.2 109.9 %spread_exchange.1 = bf16[4,8,8,128,128]{4,3,2,1,0:T(8,128)(2,1)} custom-call(bf16[2,4,256,2048]{3,2,1,0:T(8,128)(2,1)} %strengths.1, bf16[2,4,256,128]{3,2,1,0:T(8,128)(2,1)S(1)} %bitcast.6, bf16[2048,1024]{1,0:T(8,128)(2,1)S(1)} %copy-done, bf16[128,1024]{1,0:T(8,128)(2,1)S(1)} %copy-done.1), custom_call_target="tpu_custom_call" | custom-call | tf_op jit(solution)/shard_map/spread_exchange/pallas_call | solution.py:191
  127.0 17.0 %transform.1 = f32[2,8,16,2,32,128]{5,4,3,2,1,0:T(8,128)} custom-call(bf16[4,8,8,2,4,16,128]{6,5,4,3,2,1,0:T(8,128)(2,1)} %bitcast.8, f32[32,128]{1,0:T(8,128)} %constant.46.clone.tc_ref, f32[32,128]{1,0:T(8,128)} %constant.47.clone.ts_ref, bf16[256,256]{1,0:T(8,128)(2,1)} %constant.48.clone.hi_ref), custom_call_target="tpu_custom_call" | custom-call | tf_op jit(solution)/shard_map/transform/pallas_call | solution.py:268
  (6 shorter events, 0.1 us)
Async XLA Ops:
  0.0 15.0 %copy-start.1 = (bf16[128,1024]{1,0:T(8,128)(2,1)S(1)}, bf16[128,1024]{1,0:T(8,128)(2,1)}, u32[]{:S(2)}) copy-start(bf16[128,1024]{1,0:T(8,128)(2,1)} %constant.45.clone.select) | copy-start | bytes 786436
  0.0 8.3 %copy-start.2 = (f32[2048]{0:T(1024)S(1)}, f32[2048]{0:T(1024)}, u32[]{:S(2)}) copy-start(f32[2048]{0:T(1024)} %param.9) | copy-start | bytes 24580
  6.5 8.0 %collective-permute-start = (f32[4,2048]{1,0:T(4,128)S(1)}, f32[4,2048]{1,0:T(4,128)S(1)}, u32[]{:S(2)}, u32[]{:S(2)}) collective-permute-start(f32[4,2048]{1,0:T(4,128)S(1)} %get-tuple-element.8), channel_id=1, source_target_pairs={{0,2},{2,4},{4,6},{6,8},{8,10},{10,12},{12,14},{14,16},{16,18},{18... | collective-permute-start | bytes 98312 | tf_op jit(solution)/shard_map/ppermute | solution.py:314
  8.3 6.2 %collective-permute-start.1 = (f32[4,2048]{1,0:T(4,128)S(1)}, f32[4,2048]{1,0:T(4,128)S(1)}, u32[]{:S(2)}, u32[]{:S(2)}) collective-permute-start(f32[4,2048]{1,0:T(4,128)S(1)} %get-tuple-element.9), channel_id=1, source_target_pairs={{2,0},{4,2},{6,4},{8,6},{10,8},{12,10},{14,12},{16,14},{18,16},{20... | collective-permute-start | bytes 98312 | tf_op jit(solution)/shard_map/ppermute | solution.py:315
  15.0 2.2 %copy-start = (bf16[2048,1024]{1,0:T(8,128)(2,1)S(1)}, bf16[2048,1024]{1,0:T(8,128)(2,1)}, u32[]{:S(2)}) copy-start(bf16[2048,1024]{1,0:T(8,128)(2,1)} %select_convert_fusion.table) | copy-start | bytes 12582916
where the time goes:
time: 146 us; the launch traced here: 144 us
  Pallas kernels  127 us (87%)
  other arithmetic  6.98 us (5%)
  matrix products  5.67 us (4%)
  local copies, waits for them, and re-layouts  2.6 us (2%)
  starting transfers between devices  1.83 us (1%)
    pallas_call x1, Pallas kernels, exchange(): pl.pallas_call(functools.partial(exchange_kernel, n_tm, n_fq), out_shape=...  110 us
    pallas_call x1, Pallas kernels, transform(): pl.pallas_call(transform_kernel, out_shape=jax.ShapeDtypeStruct((2, n_fq...  17 us
    convert_element_type x1, other arithmetic, tap_table(): return jnp.where(inside, values, 0.0).astype(jnp.bfloat16)  6.16 us
    dot_general x1, matrix products, shards(): lax.dot_general(edge_table, strengths.reshape(parts * groups * channels,...  5.67 us
  transfers between devices with their start and end apart: 2, of which 0 were waited for; matrix products, arithmetic and copies ran while one was open for 4% of the time, Pallas kernels for 0%

commit v1 on v0

v1 whole, which is shorter than its diff:
```python
import functools
import math

import jax
import jax.numpy as jnp
import numpy as np
from jax import lax
from jax.experimental import pallas as pl
from jax.experimental.pallas import tpu as pltpu
from jax.sharding import PartitionSpec as P

TAPS = 8
HALF = TAPS // 2
GRID_DEV = 1024
FFT_LO = 32
FFT_HI = 128
FFTLEN = 4096
SHARP = 0.3
MESH = pl.DeviceIdType.MESH
LANES = 128
SLABS = GRID_DEV // LANES
INNER = SLABS - 2
PER_FRAME = FFTLEN // GRID_DEV
EARLY = 3
PLACE = [INNER] + list(range(INNER)) + [INNER + 1]


def fft_list(re, im):
    n = len(re)
    if n == 1:
        return re, im
    er, ei = fft_list(re[0::2], im[0::2])
    orr, oi = fft_list(re[1::2], im[1::2])
    out_r, out_i = [None] * n, [None] * n
    for k in range(n // 2):
        c, s = math.cos(2 * math.pi * k / n), math.sin(2 * math.pi * k / n)
        a, b = orr[k], oi[k]
        if k == 0:
            tr, ti = a, b
        elif 4 * k == n:
            tr, ti = b, -a
        elif 8 * k == n:
            tr, ti = (a + b) * c, (b - a) * c
        elif 8 * k == 3 * n:
            tr, ti = (b - a) * s, -(a + b) * s
        else:
            tr, ti = a * c + b * s, b * c - a * s
        out_r[k], out_i[k] = er[k] + tr, ei[k] + ti
        out_r[k + n // 2], out_i[k + n // 2] = er[k] - tr, ei[k] - ti
    return out_r, out_i


def spread_order(count):
    bits = count.bit_length() - 1
    if 1 << bits != count:
        return list(range(count))
    return [int(format(i, "0%db" % bits)[::-1], 2) if bits else 0 for i in range(count)]


def main_kernel(
    n_tm, n_fq, strengths, cell, frac, tc, ts, hi, y,
    xv, cols, fracs, inner_table, edge_table, edge_acc, edge_out, halo, src, recv, lhs,
    load, send, arrive, halo_send, halo_arrive,
):
    t = lax.axis_index("tm")
    f = lax.axis_index("freq")
    groups = xv.shape[0]
    chunk, samples = xv.shape[3], xv.shape[4]
    rows = src.shape[3]
    span = n_tm // n_fq
    frames = span // PER_FRAME
    slot = lax.rem(t, span)
    home = lax.div(t, span)
    half = n_tm // 2
    block = half * rows
    upper = lax.div(t, half)
    quarter = lax.div(t, n_tm // 4)
    outer = (quarter == 0) | (quarter == 3)
    right = lax.rem(t + 1, n_tm)
    left = lax.rem(t + n_tm - 1, n_tm)
    steps = 2 * groups
    early = min(EARLY, steps)
    keep = home == f

    def order(k):
        far = jnp.where(outer, lax.div(k, groups), 1 - lax.rem(k, 2))
        side = jnp.where(far == 1, 1 - upper, upper)
        return side, jnp.where(outer, lax.rem(k, groups), lax.div(k, 2))

    def fetch(g, d):
        channels = pl.ds(pl.multiple_of(d * chunk, chunk), chunk)
        return pltpu.make_async_copy(strengths.at[:, g, channels, :], xv.at[g, d], load.at[g, d])

    def fetch_step(k, c):
        side, g = order(k)

        def one(i, c):
            fetch(g, side * half + i).start()
            return c

        return lax.fori_loop(0, half, one, c)

    lax.fori_loop(0, steps, fetch_step, 0)

    def loaded(k):
        side, g = order(k)

        def one(i, c):
            fetch(g, side * half + i).wait()
            return c

        lax.fori_loop(0, half, one, 0)

    barrier = pltpu.get_barrier_semaphore()

    def greet(i, c):
        origin = f * span + lax.rem(slot + 1 + i, span)

        def one(j, c):
            other = lax.rem(f + j, n_fq)

            @pl.when((origin != t) | (other != f))
            def _():
                pl.semaphore_signal(barrier, inc=1, device_id=(origin, other), device_id_type=MESH)

            return c

        return lax.fori_loop(0, n_fq, one, c)

    lax.fori_loop(0, span, greet, 0)
    for peer in (left, right):
        pl.semaphore_signal(barrier, inc=1, device_id=(peer, f), device_id_type=MESH)

    base = t * GRID_DEV
    for i in range(samples // LANES):
        at = pl.ds(i * LANES, LANES)
        local = (cell[i : i + 1, :] - base).astype(jnp.float32)
        cols[at, :] = jnp.broadcast_to(local, (LANES, LANES)).T
        fracs[at, :] = jnp.broadcast_to(frac[i : i + 1, :], (LANES, LANES)).T
    lane = lax.broadcasted_iota(jnp.int32, (LANES, LANES), 1)

    def build(table, place, columns):
        def part(i, c):
            at = pl.ds(pl.multiple_of(i * LANES, LANES), LANES)
            d = columns - cols[at, :]
            u = d - fracs[at, :]
            w = jnp.exp(-SHARP * (u * u))
            inside = jnp.abs(d - 0.5) < float(HALF)
            table[at, place * LANES : (place + 1) * LANES] = jnp.where(inside, w, 0.0).astype(jnp.bfloat16)
            return c

        lax.fori_loop(0, samples // LANES, part, 0)

    def slab_columns(j):
        return (lane + j * LANES).astype(jnp.float32)

    def operand(k):
        side, g = order(k)
        return xv[g, pl.ds(side * half, half)].reshape(block, samples)

    def grid_inner(k, first, count):
        side, g = order(k)
        acc = jnp.dot(
            operand(k),
            inner_table[:, first * LANES : (first + count) * LANES],
            preferred_element_type=jnp.float32,
        ).astype(jnp.bfloat16)
        for i in range(half):
            for j in range(count):
                src[side * half + i, g, first + j] = acc[
                    i * rows : (i + 1) * rows, j * LANES : (j + 1) * LANES
                ]

    def copy_out(d, g, first, count):
        part = pl.ds(first, count)
        return pltpu.make_async_remote_copy(
            src_ref=src.at[d, g, part],
            dst_ref=recv.at[f, slot, g, part],
            send_sem=send.at[d, g],
            recv_sem=arrive.at[f, slot, g],
            device_id=(d, home),
            device_id_type=MESH,
        )

    spread = spread_order(half)

    def send_step(k, first, count):
        side, g = order(k)
        for i in range(half):
            d = side * half + lax.rem(t + spread[i], half)

            @pl.when((d != t) | (home != f))
            def _():
                copy_out(d, g, first, count).start()

    loaded(0)
    for b in range(INNER // 2):
        for j in range(2):
            build(inner_table, 2 * b + j, slab_columns(1 + 2 * b + j))
        grid_inner(0, 2 * b, 2)
        if b == 0:
            pl.semaphore_wait(barrier, jnp.where(keep, n_tm + 1, n_tm + 2))
        send_step(0, 2 * b, 2)

    beyond = jnp.where(
        lane < HALF, lane + GRID_DEV, jnp.where((lane >= 16 - HALF) & (lane < 16), lane - 16, -GRID_DEV)
    ).astype(jnp.float32)
    build(edge_table, 0, slab_columns(0))
    build(edge_table, 1, slab_columns(SLABS - 1))
    build(edge_table, 2, beyond)

    def row_block(k):
        side, g = order(k)
        return pl.ds(pl.multiple_of((g * 2 + side) * block, LANES), block)

    def edges(k, c):
        @pl.when(k > 0)
        def _():
            loaded(k)

        at = row_block(k)
        acc = jnp.dot(operand(k), edge_table[...], preferred_element_type=jnp.float32)
        edge_acc[at, :] = acc[:, : 2 * LANES]
        edge_out[:, at] = acc[:, 2 * LANES :].T[:16]
        return c

    lax.fori_loop(0, steps, edges, 0)
    halo[8 : LANES - 8, :] = jnp.zeros((LANES - 16, halo.shape[1]), jnp.float32)

    def halo_copy(i, peer):
        return pltpu.make_async_remote_copy(
            src_ref=edge_out.at[8 * i : 8 * i + 8],
            dst_ref=halo.at[pl.ds(i * (LANES - 8), 8)],
            send_sem=halo_send.at[i],
            recv_sem=halo_arrive.at[i],
            device_id=(peer, f),
            device_id_type=MESH,
        )

    halo_copy(0, right).start()
    halo_copy(1, left).start()

    def early_step(k, c):
        grid_inner(k, 0, INNER)
        send_step(k, 0, INNER)
        return c

    lax.fori_loop(1, early, early_step, 0)
    halo_copy(0, right).wait_recv()
    halo_copy(1, left).wait_recv()

    def finish_edges(k):
        side, g = order(k)
        at = row_block(k)
        acc = edge_acc[at, :]
        outside = halo[:, at].T
        spot = lax.broadcasted_iota(jnp.int32, (block, LANES), 1)
        low = acc[:, :LANES] + jnp.where(spot < LANES // 2, outside, 0.0)
        high = acc[:, LANES:] + jnp.where(spot >= LANES // 2, outside, 0.0)
        low, high = low.astype(jnp.bfloat16), high.astype(jnp.bfloat16)
        for i in range(half):
            src[side * half + i, g, INNER] = low[i * rows : (i + 1) * rows]
            src[side * half + i, g, INNER + 1] = high[i * rows : (i + 1) * rows]

    def early_edges(k, c):
        finish_edges(k)
        send_step(k, INNER, 2)
        return c

    lax.fori_loop(0, early, early_edges, 0)

    def late_step(k, c):
        grid_inner(k, 0, INNER)
        finish_edges(k)
        send_step(k, 0, SLABS)
        return c

    lax.fori_loop(early, steps, late_step, 0)

    @pl.when(keep)
    def _():
        def own(g, c):
            recv[f, slot, g] = src[t, g]
            return c

        lax.fori_loop(0, groups, own, 0)

    def landed(g, source, s):
        return pltpu.make_async_remote_copy(
            src_ref=src.at[0, g],
            dst_ref=recv.at[source, s, g],
            send_sem=send.at[0, g],
            recv_sem=arrive.at[source, s, g],
            device_id=(t, f),
            device_id_type=MESH,
        )

    flat = y.reshape(2, n_fq * groups, chunk * frames * FFT_LO, FFT_HI)

    def unit(i, c):
        turn = lax.div(i, groups * n_fq)
        m = lax.rem(turn + frames - 1 + f, frames)
        g = lax.rem(lax.div(i, n_fq), groups)
        source = lax.rem(f + lax.rem(i, n_fq), n_fq)

        def await_one(s, c):
            slot_in = m * PER_FRAME + s

            @pl.when((source != f) | (f * span + slot_in != t))
            def _():
                landed(g, source, slot_in).wait_recv()

            return c

        lax.fori_loop(0, PER_FRAME, await_one, 0)
        re, im = [], []
        for n in range(FFT_LO):
            tile = recv.at[source, m * PER_FRAME + n // SLABS, g, PLACE[n % SLABS]]
            re.append(tile[:chunk].astype(jnp.float32))
            im.append(tile[chunk:].astype(jnp.float32))
        re, im = fft_list(re, im)
        for a in range(FFT_LO):
            cc = tc[a : a + 1, :]
            ss = ts[a : a + 1, :]
            at = pl.ds(a * chunk, chunk)
            lhs[at, :FFT_HI] = (re[a] * cc + im[a] * ss).astype(jnp.bfloat16)
            lhs[at, FFT_HI:] = (im[a] * cc - re[a] * ss).astype(jnp.bfloat16)
        out = jnp.dot(lhs[...], hi[...], preferred_element_type=jnp.float32)
        for a in range(FFT_LO):
            for p in range(2):
                flat[p, source * groups + g, pl.ds(m * FFT_LO + a, chunk, stride=frames * FFT_LO), :] = out[
                    a * chunk : (a + 1) * chunk, p * FFT_HI : (p + 1) * FFT_HI
                ]
        return c

    lax.fori_loop(0, frames * groups * n_fq, unit, 0)

    def sent(i, c):
        d, g = lax.div(i, groups), lax.rem(i, groups)

        @pl.when((d != t) | (home != f))
        def _():
            copy_out(d, g, 0, SLABS).wait_send()

        return c

    lax.fori_loop(0, n_tm * groups, sent, 0)
    halo_copy(0, right).wait_send()
    halo_copy(1, left).wait_send()


def write_kernel(y, out, sems):
    parts, blocks = y.shape[0], y.shape[1]

    def copies():
        return [
            pltpu.make_async_copy(y.at[p, b], out.at[p, b], sems.at[p * blocks + b])
            for p in range(parts)
            for b in range(blocks)
        ]

    for c in copies():
        c.start()
    for c in copies():
        c.wait()


def shards(strengths, sample_cell, sample_frac):
    n_tm, n_fq = lax.axis_size("tm"), lax.axis_size("freq")
    parts, groups, channels, samples = strengths.shape
    span = n_tm // n_fq
    frames = span // PER_FRAME
    chunk = channels // n_tm
    rows = parts * chunk
    total = groups * n_tm * rows
    low = np.arange(FFT_LO)[:, None] * np.arange(FFT_HI)[None, :] * (2 * math.pi / FFTLEN)
    high = np.arange(FFT_HI)[:, None] * np.arange(FFT_HI)[None, :] % FFT_HI * (2 * math.pi / FFT_HI)
    hc, hs = np.cos(high), np.sin(high)
    full = np.block([[hc, -hs], [hs, hc]]).astype(np.float32) / math.sqrt(FFTLEN)
    vmem = pl.BlockSpec(memory_space=pltpu.VMEM)
    y_shape = (parts, n_fq * groups, chunk, frames, FFT_LO, FFT_HI)
    y = pl.pallas_call(
        functools.partial(main_kernel, n_tm, n_fq),
        out_shape=jax.ShapeDtypeStruct(y_shape, jnp.float32),
        in_specs=[pl.BlockSpec(memory_space=pl.ANY)] + [vmem] * 5,
        out_specs=vmem,
        scratch_shapes=[
            pltpu.VMEM((groups, n_tm, parts, chunk, samples), jnp.bfloat16),
            pltpu.VMEM((samples, LANES), jnp.float32),
            pltpu.VMEM((samples, LANES), jnp.float32),
            pltpu.VMEM((samples, INNER * LANES), jnp.bfloat16),
            pltpu.VMEM((samples, 3 * LANES), jnp.bfloat16),
            pltpu.VMEM((total, 2 * LANES), jnp.float32),
            pltpu.VMEM((16, total), jnp.float32),
            pltpu.VMEM((LANES, total), jnp.float32),
            pltpu.VMEM((n_tm, groups, SLABS, rows, LANES), jnp.bfloat16),
            pltpu.VMEM((n_fq, span, groups, SLABS, rows, LANES), jnp.bfloat16),
            pltpu.VMEM((FFT_LO * chunk, 2 * FFT_HI), jnp.bfloat16),
            pltpu.SemaphoreType.DMA((groups, n_tm)),
            pltpu.SemaphoreType.DMA((n_tm, groups)),
            pltpu.SemaphoreType.DMA((n_fq, span, groups)),
            pltpu.SemaphoreType.DMA((2,)),
            pltpu.SemaphoreType.DMA((2,)),
        ],
        compiler_params=pltpu.CompilerParams(
            collective_id=0, has_side_effects=True, vmem_limit_bytes=46 * 1024 * 1024
        ),
        name="grid_exchange_transform",
    )(
        strengths,
        sample_cell.reshape(samples // LANES, LANES),
        sample_frac.reshape(samples // LANES, LANES),
        jnp.asarray(np.cos(low), jnp.float32),
        jnp.asarray(np.sin(low), jnp.float32),
        jnp.asarray(full.astype(jnp.bfloat16)),
    )
    return pl.pallas_call(
        write_kernel,
        out_shape=jax.ShapeDtypeStruct(y_shape, jnp.float32),
        in_specs=[vmem],
        out_specs=pl.BlockSpec(memory_space=pl.ANY),
        scratch_shapes=[pltpu.SemaphoreType.DMA((parts * n_fq * groups,))],
        compiler_params=pltpu.CompilerParams(vmem_limit_bytes=16 * 1024 * 1024),
        name="write_out",
    )(y)


def solution(mesh):
    placed = (P(None, "freq", None, "tm"), P("tm"), P("tm"))
    return jax.shard_map(
        shards,
        mesh=mesh,
        in_specs=placed,
        out_specs=P(None, None, "tm", "freq", None, None),
        check_vma=False,
    )
```

time: 146 us -> 127 us (0.87); the launches traced: 144 us -> 127 us
  Pallas kernels: 127 us -> 119 us
  other arithmetic: 6.98 us -> 0 us
  matrix products: 5.67 us -> 0 us
  local copies, waits for them, and re-layouts: 2.6 us -> 7.11 us
  starting transfers between devices: 1.83 us -> 0 us
    pallas_call x2, Pallas kernels: 127 us -> 119 us  [the longest x1 116 us: shards(): pl.pallas_call(functools.partial(main_kernel, n_tm, n_fq), out_shape=jax....]
    convert_element_type x1 -> x0, other arithmetic: 6.16 us -> none  [tap_table(): return jnp.where(inside, values, 0.0).astype(jnp.bfloat16)]
    dot_general x1 -> x0, matrix products: 5.67 us -> none  [shards(): lax.dot_general(edge_table, strengths.reshape(parts * groups * channels,...]
    unnamed x7 -> x12, local copies, waits for them, and re-layouts: 2.46 us -> 7.11 us
    ppermute x2 -> x0, starting transfers between devices: 1.83 us -> none  [the longest x1 1.82 us: shards(): lax.ppermute(edges[HALF:], 'tm', [(i, (i + 1) % n_tm) for i in range(n_tm)])]
  transfers between devices with their start and end apart: 2 -> 0, of which waited for: 0 -> 0; matrix products, arithmetic and copies ran while one was open for 4% -> 0% of each run, Pallas kernels for 0% -> 0%
where the time goes in v1:
time: 127 us
  Pallas kernels  119 us (94%)
  local copies, waits for them, and re-layouts  7.11 us (6%)
    pallas_call x1, Pallas kernels, shards(): pl.pallas_call(functools.partial(main_kernel, n_tm, n_fq), out_shape=jax....  116 us
    unnamed x12, local copies, waits for them, and re-layouts  7.11 us
    pallas_call x1, Pallas kernels, shards(): pl.pallas_call(write_kernel, out_shape=jax.ShapeDtypeStruct(y_shape, jnp....  3.41 us

profile of v1, /device:TPU:5, one launch (start us, length us, event | category | flops | bytes accessed | tf_op | source)
XLA Modules:
  0.0 126.5 jit_solution(16762135304481796703)
XLA Ops:
  0.0 0.0 copy-start.1
  0.0 0.9 copy-done.1
  0.9 0.0 copy-start.2
  0.9 0.7 copy-done.2
  1.6 0.0 copy-start.3
  1.6 0.7 copy-done.3
  2.3 0.0 copy-start.4
  2.3 0.7 copy-done.4
  3.0 0.0 copy-start.5
  3.0 0.7 copy-done.5
  3.7 116.0 %grid_exchange_transform.1.y = f32[2,8,16,2,32,128]{5,4,3,2,1,0:T(8,128)} custom-call(bf16[2,4,256,2048]{3,2,1,0:T(8,128)(2,1)} %strengths.1, s32[16,128]{1,0:T(8,128)S(1)} %bitcast.2, f32[16,128]{1,0:T(8,128)S(1)} %bitcast.3, f32[32,128]{1,0:T(8,128)S(1)} %copy-done.3, f32[32,128]{1,0:T(8,128)S(1)} %copy-done.2, bf16[256,256]{1,0:T(8,128)(2,1)S(1)} %copy-done.1), custom_call_target="tpu_custom_call" | custom-call | tf_op jit(solution)/shard_map/grid_exchange_transform/pallas_call | solution.py:382
  119.7 0.0 copy-start
  119.8 3.4 %copy-done = f32[2,8,16,2,32,128]{5,4,3,2,1,0:T(8,128)S(1)} copy-done((f32[2,8,16,2,32,128]{5,4,3,2,1,0:T(8,128)S(1)}, f32[2,8,16,2,32,128]{5,4,3,2,1,0:T(8,128)}, u32[]{:S(2)}) %copy-start) | copy-done | bytes 8388632
  123.1 3.4 %write_out.1 = f32[2,8,16,2,32,128]{5,4,3,2,1,0:T(8,128)} custom-call(f32[2,8,16,2,32,128]{5,4,3,2,1,0:T(8,128)S(1)} %copy-done), custom_call_target="tpu_custom_call" | custom-call | tf_op jit(solution)/shard_map/write_out/pallas_call | solution.py:417
Async XLA Ops:
  0.0 0.9 copy-start.1
  0.9 0.7 copy-start.2
  1.6 0.7 copy-start.3
  2.3 0.7 copy-start.4
  3.0 0.7 copy-start.5
  119.7 3.4 %copy-start = (f32[2,8,16,2,32,128]{5,4,3,2,1,0:T(8,128)S(1)}, f32[2,8,16,2,32,128]{5,4,3,2,1,0:T(8,128)}, u32[]{:S(2)}) copy-start(f32[2,8,16,2,32,128]{5,4,3,2,1,0:T(8,128)} %grid_exchange_transform.1.y) | copy-start | bytes 25165828

commit v2 on v1

v2 whole, which is shorter than its diff:
```python
import functools
import math

import jax
import jax.numpy as jnp
import numpy as np
from jax import lax
from jax.experimental import pallas as pl
from jax.experimental.pallas import tpu as pltpu
from jax.sharding import PartitionSpec as P

TAPS = 8
HALF = TAPS // 2
GRID_DEV = 1024
FFT_LO = 32
FFT_HI = 128
FFTLEN = 4096
SHARP = 0.3
MESH = pl.DeviceIdType.MESH
LANES = 128
SLABS = GRID_DEV // LANES
INNER = SLABS - 2
PER_FRAME = FFTLEN // GRID_DEV
EARLY = 3
FIRST = ((0, 2), (2, 4))
PLACE = [INNER] + list(range(INNER)) + [INNER + 1]


def fft_list(re, im):
    n = len(re)
    if n == 1:
        return re, im
    er, ei = fft_list(re[0::2], im[0::2])
    orr, oi = fft_list(re[1::2], im[1::2])
    out_r, out_i = [None] * n, [None] * n
    for k in range(n // 2):
        c, s = math.cos(2 * math.pi * k / n), math.sin(2 * math.pi * k / n)
        a, b = orr[k], oi[k]
        if k == 0:
            tr, ti = a, b
        elif 4 * k == n:
            tr, ti = b, -a
        elif 8 * k == n:
            tr, ti = (a + b) * c, (b - a) * c
        elif 8 * k == 3 * n:
            tr, ti = (b - a) * s, -(a + b) * s
        else:
            tr, ti = a * c + b * s, b * c - a * s
        out_r[k], out_i[k] = er[k] + tr, ei[k] + ti
        out_r[k + n // 2], out_i[k + n // 2] = er[k] - tr, ei[k] - ti
    return out_r, out_i


def spread_order(count):
    bits = count.bit_length() - 1
    if 1 << bits != count:
        return list(range(count))
    return [int(format(i, "0%db" % bits)[::-1], 2) if bits else 0 for i in range(count)]


def main_kernel(
    n_tm, n_fq, strengths, cell_hbm, frac_hbm, tc_hbm, ts_hbm, hi_hbm, y,
    xv, cell, frac, tc, ts, hi, cols, fracs, table, edge_out, halo, src, recv, lhs,
    small, load, send, arrive, halo_send, halo_arrive,
):
    t = lax.axis_index("tm")
    f = lax.axis_index("freq")
    parts, groups, channels, samples = xv.shape
    chunk = channels // n_tm
    rows = src.shape[3]
    wide = channels // 2
    both = 2 if groups % 2 == 0 else 1
    span = n_tm // n_fq
    frames = span // PER_FRAME
    slot = lax.rem(t, span)
    home = lax.div(t, span)
    half = n_tm // 2
    block = half * rows
    upper = lax.div(t, half)
    quarter = lax.div(t, n_tm // 4)
    outer = (quarter == 0) | (quarter == 3)
    right = lax.rem(t + 1, n_tm)
    left = lax.rem(t + n_tm - 1, n_tm)
    steps = 2 * groups
    early = min(EARLY, steps)
    keep = home == f

    def order(k):
        ahead = (k == 0) | ((lax.rem(k, 2) == 1) & (k < steps - 1))
        far = jnp.where(outer, k >= groups, ahead)
        inward = jnp.where(ahead, lax.div(k + 1, 2), lax.div(k - 1, 2))
        side = jnp.where(far, 1 - upper, upper)
        return side, jnp.where(outer, lax.rem(k, groups), inward)

    constants = [
        pltpu.make_async_copy(a, b, small.at[i])
        for i, (a, b) in enumerate(
            ((cell_hbm, cell), (frac_hbm, frac), (tc_hbm, tc), (ts_hbm, ts), (hi_hbm, hi))
        )
    ]
    for i in range(2):
        constants[i].start()

    def fetch(k):
        side, g = order(k)
        at = (slice(None), g, pl.ds(pl.multiple_of(side * wide, wide), wide))
        return pltpu.make_async_copy(strengths.at[at], xv.at[at], load.at[k])

    fetch(0).start()

    barrier = pltpu.get_barrier_semaphore()

    def greet(i, c):
        origin = f * span + lax.rem(slot + 1 + i, span)

        def one(j, c):
            other = lax.rem(f + j, n_fq)

            @pl.when((origin != t) | (other != f))
            def _():
                pl.semaphore_signal(barrier, inc=1, device_id=(origin, other), device_id_type=MESH)

            return c

        return lax.fori_loop(0, n_fq, one, c)

    lax.fori_loop(0, span, greet, 0)
    for peer in (left, right):
        pl.semaphore_signal(barrier, inc=1, device_id=(peer, f), device_id_type=MESH)

    for k in range(1, steps):
        fetch(k).start()

    base = t * GRID_DEV
    constants[0].wait()
    constants[1].wait()
    for i in range(samples // LANES):
        at = pl.ds(i * LANES, LANES)
        local = (cell[i : i + 1, :] - base).astype(jnp.float32)
        cols[at, :] = jnp.broadcast_to(local, (LANES, LANES)).T
        fracs[at, :] = jnp.broadcast_to(frac[i : i + 1, :], (LANES, LANES)).T
    lane = lax.broadcasted_iota(jnp.int32, (LANES, LANES), 1)

    def build(place, columns):
        def part(i, c):
            at = pl.ds(pl.multiple_of(i * LANES, LANES), LANES)
            d = columns - cols[at, :]
            u = d - fracs[at, :]
            w = jnp.exp(-SHARP * (u * u))
            inside = jnp.abs(d - 0.5) < float(HALF)
            table[at, place * LANES : (place + 1) * LANES] = jnp.where(inside, w, 0.0).astype(jnp.bfloat16)
            return c

        lax.fori_loop(0, samples // LANES, part, 0, unroll=4)

    def slab_columns(j):
        return (lane + j * LANES).astype(jnp.float32)

    def operand(k):
        side, g = order(k)
        at = pl.ds(pl.multiple_of(side * wide, wide), wide)
        return xv[:, g, at, :].reshape(block, samples)

    def product(k, first, count):
        return jnp.dot(
            operand(k),
            table[:, first * LANES : (first + count) * LANES],
            preferred_element_type=jnp.float32,
        )

    def put(k, first, pieces):
        side, g = order(k)
        for j, part in enumerate(pieces):
            part = part.astype(jnp.bfloat16)
            for i in range(half):
                for p in range(parts):
                    start = p * wide + i * chunk
                    src[side * half + i, g, first + j, p * chunk : (p + 1) * chunk] = part[start : start + chunk]

    def slabs(acc):
        return [acc[:, j : j + LANES] for j in range(0, acc.shape[1], LANES)]

    def with_halo(k, low, high):
        side, g = order(k)
        outside = jnp.concatenate(
            [
                halo[:, pl.ds(pl.multiple_of(g * 2 * block + p * channels + side * wide, LANES), wide)].T
                for p in range(parts)
            ]
        )
        spot = lax.broadcasted_iota(jnp.int32, (block, LANES), 1)
        return [
            low + jnp.where(spot < LANES // 2, outside, 0.0),
            high + jnp.where(spot >= LANES // 2, outside, 0.0),
        ]

    def copy_out(d, g, first, count, pair=1):
        part = (pl.ds(g, pair), pl.ds(first, count))
        return pltpu.make_async_remote_copy(
            src_ref=src.at[(d,) + part],
            dst_ref=recv.at[(f, slot) + part],
            send_sem=send.at[d, g],
            recv_sem=arrive.at[f, slot, g],
            device_id=(d, home),
            device_id_type=MESH,
        )

    spread = spread_order(half)

    def send_step(k, first, count, pair=1):
        side, g = order(k)
        for i in range(half):
            d = side * half + lax.rem(t + spread[i], half)

            @pl.when((d != t) | (home != f))
            def _():
                copy_out(d, g - (pair - 1), first, count, pair).start()

    fetch(0).wait()
    with jax.named_scope("first"):
        for first, count in FIRST:
            for j in range(first, first + count):
                build(j, slab_columns(1 + j))
            put(0, first, slabs(product(0, first, count)))
            if first == 0:
                pl.semaphore_wait(barrier, jnp.where(keep, n_tm + 1, n_tm + 2))
            send_step(0, first, count)
            if first == 0:
                for i in range(2, 5):
                    constants[i].start()

    beyond = jnp.where(
        lane < HALF, lane + GRID_DEV, jnp.where((lane >= 16 - HALF) & (lane < 16), lane - 16, -GRID_DEV)
    ).astype(jnp.float32)

    def edges(g, c):
        acc = jnp.dot(
            xv[:, g].reshape(2 * block, samples),
            table[:, SLABS * LANES :],
            preferred_element_type=jnp.float32,
        )
        edge_out[:, pl.ds(pl.multiple_of(g * 2 * block, LANES), 2 * block)] = acc.T[:16]
        return c

    with jax.named_scope("edges"):
        build(SLABS, beyond)
        for k in range(1, steps):
            fetch(k).wait()
        lax.fori_loop(0, groups, edges, 0)
        halo[8 : LANES - 8, :] = jnp.zeros((LANES - 16, halo.shape[1]), jnp.float32)

    def halo_copy(i, peer):
        return pltpu.make_async_remote_copy(
            src_ref=edge_out.at[8 * i : 8 * i + 8],
            dst_ref=halo.at[pl.ds(i * (LANES - 8), 8)],
            send_sem=halo_send.at[i],
            recv_sem=halo_arrive.at[i],
            device_id=(peer, f),
            device_id_type=MESH,
        )

    halo_copy(0, right).start()
    halo_copy(1, left).start()

    def early_step(k, c):
        put(k, 0, slabs(product(k, 0, INNER)))
        send_step(k, 0, INNER)
        return c

    with jax.named_scope("early"):
        lax.fori_loop(1, early, early_step, 0)
        build(INNER, slab_columns(0))
        build(INNER + 1, slab_columns(SLABS - 1))
    with jax.named_scope("halo_wait"):
        halo_copy(0, right).wait_recv()
        halo_copy(1, left).wait_recv()

    def early_edges(k, c):
        put(k, INNER, with_halo(k, *slabs(product(k, INNER, 2))))
        send_step(k, INNER, 2)
        return c

    def late_step(k, c):
        pieces = slabs(product(k, 0, SLABS))
        put(k, 0, pieces[:INNER] + with_halo(k, *pieces[INNER:]))
        if both == 1:
            send_step(k, 0, SLABS)
        else:
            in_pairs = outer & (k >= groups)

            @pl.when(in_pairs & (lax.rem(k, 2) == 1))
            def _():
                send_step(k, 0, SLABS, both)

            @pl.when(jnp.logical_not(in_pairs))
            def _():
                send_step(k, 0, SLABS)

        return c

    with jax.named_scope("early_edges"):
        lax.fori_loop(0, early, early_edges, 0)
    with jax.named_scope("late"):
        lax.fori_loop(early, steps, late_step, 0)

    @pl.when(keep)
    def _():
        def own(g, c):
            recv[f, slot, g] = src[t, g]
            return c

        lax.fori_loop(0, groups, own, 0)

    def landed(source, s, g, pair=1):
        return pltpu.make_async_remote_copy(
            src_ref=src.at[0, pl.ds(g, pair)],
            dst_ref=recv.at[source, s, pl.ds(g, pair)],
            send_sem=send.at[0, g],
            recv_sem=arrive.at[source, s, g],
            device_id=(t, f),
            device_id_type=MESH,
        )

    def is_outer(index):
        q = lax.div(index, n_tm // 4)
        return (q == 0) | (q == 3)

    def paired(origin, d):
        return is_outer(origin) & (lax.div(origin, half) != lax.div(d, half)) & (both == 2)

    for i in range(2, 5):
        constants[i].wait()
    flat = y.reshape(2, n_fq * groups, chunk * frames * FFT_LO, FFT_HI)
    ready = min(2, groups)
    turns = frames * groups

    def sent(i, c):
        d, g = lax.div(i, groups), lax.rem(i, groups)
        away = (d != t) | (home != f)
        two = paired(t, d)

        @pl.when(away & jnp.logical_not(two))
        def _():
            copy_out(d, g, 0, SLABS).wait_send()

        if both == 2:

            @pl.when(away & two & (lax.rem(g, 2) == 0))
            def _():
                copy_out(d, g, 0, SLABS, both).wait_send()

        return c

    def unit(i, c):
        n = lax.div(i, n_fq)
        source = lax.rem(f + lax.rem(i, n_fq), n_fq)
        late = n - (turns - groups)
        first = n < ready
        last = (late >= ready) & (late >= 0)
        inward = first | last
        g = jnp.where(first, n, jnp.where(last, late, lax.rem(n - ready, groups)))
        m = jnp.where(inward, 0, 1 + lax.div(n - ready, groups))
        m = lax.rem(m + frames - 1 + f, frames)

        def await_one(s, c):
            slot_in = m * PER_FRAME + s
            origin = f * span + slot_in
            away = (source != f) | (origin != t)
            two = paired(origin, t)

            @pl.when(away & jnp.logical_not(two))
            def _():
                landed(source, slot_in, g).wait_recv()

            if both == 2:

                @pl.when(away & two & (lax.rem(g, 2) == 0))
                def _():
                    landed(source, slot_in, g, both).wait_recv()

            return c

        with jax.named_scope("await"):
            lax.fori_loop(0, PER_FRAME, await_one, 0)
        re, im = [], []
        for n in range(FFT_LO):
            tile = recv.at[source, m * PER_FRAME + n // SLABS, g, PLACE[n % SLABS]]
            re.append(tile[:chunk].astype(jnp.float32))
            im.append(tile[chunk:].astype(jnp.float32))
        re, im = fft_list(re, im)
        for a in range(FFT_LO):
            cc = tc[a : a + 1, :]
            ss = ts[a : a + 1, :]
            at = pl.ds(a * chunk, chunk)
            lhs[at, :FFT_HI] = (re[a] * cc + im[a] * ss).astype(jnp.bfloat16)
            lhs[at, FFT_HI:] = (im[a] * cc - re[a] * ss).astype(jnp.bfloat16)
        out = jnp.dot(lhs[...], hi[...], preferred_element_type=jnp.float32)
        for a in range(FFT_LO):
            for p in range(2):
                flat[p, source * groups + g, pl.ds(m * FFT_LO + a, chunk, stride=frames * FFT_LO), :] = out[
                    a * chunk : (a + 1) * chunk, p * FFT_HI : (p + 1) * FFT_HI
                ]
        return c

    lax.fori_loop(0, turns * n_fq, unit, 0)
    with jax.named_scope("sent"):
        lax.fori_loop(0, n_tm * groups, sent, 0)
        halo_copy(0, right).wait_send()
        halo_copy(1, left).wait_send()


def write_kernel(y, out, sems):
    parts, blocks = y.shape[0], y.shape[1]

    def copies():
        return [
            pltpu.make_async_copy(y.at[p, b], out.at[p, b], sems.at[p * blocks + b])
            for p in range(parts)
            for b in range(blocks)
        ]

    for c in copies():
        c.start()
    for c in copies():
        c.wait()


def shards(strengths, sample_cell, sample_frac):
    n_tm, n_fq = lax.axis_size("tm"), lax.axis_size("freq")
    parts, groups, channels, samples = strengths.shape
    span = n_tm // n_fq
    frames = span // PER_FRAME
    chunk = channels // n_tm
    rows = parts * chunk
    total = groups * n_tm * rows
    low = np.arange(FFT_LO)[:, None] * np.arange(FFT_HI)[None, :] * (2 * math.pi / FFTLEN)
    high = np.arange(FFT_HI)[:, None] * np.arange(FFT_HI)[None, :] % FFT_HI * (2 * math.pi / FFT_HI)
    hc, hs = np.cos(high), np.sin(high)
    full = np.block([[hc, -hs], [hs, hc]]).astype(np.float32) / math.sqrt(FFTLEN)
    vmem = pl.BlockSpec(memory_space=pltpu.VMEM)
    y_shape = (parts, n_fq * groups, chunk, frames, FFT_LO, FFT_HI)
    y = pl.pallas_call(
        functools.partial(main_kernel, n_tm, n_fq),
        out_shape=pltpu.VMEM(y_shape, jnp.float32),
        in_specs=[pl.BlockSpec(memory_space=pltpu.HBM)] * 6,
        out_specs=vmem,
        scratch_shapes=[
            pltpu.VMEM((parts, groups, channels, samples), jnp.bfloat16),
            pltpu.VMEM((samples // LANES, LANES), jnp.int32),
            pltpu.VMEM((samples // LANES, LANES), jnp.float32),
            pltpu.VMEM((FFT_LO, FFT_HI), jnp.float32),
            pltpu.VMEM((FFT_LO, FFT_HI), jnp.float32),
            pltpu.VMEM((2 * FFT_HI, 2 * FFT_HI), jnp.bfloat16),
            pltpu.VMEM((samples, LANES), jnp.float32),
            pltpu.VMEM((samples, LANES), jnp.float32),
            pltpu.VMEM((samples, (SLABS + 1) * LANES), jnp.bfloat16),
            pltpu.VMEM((16, total), jnp.float32),
            pltpu.VMEM((LANES, total), jnp.float32),
            pltpu.VMEM((n_tm, groups, SLABS, rows, LANES), jnp.bfloat16),
            pltpu.VMEM((n_fq, span, groups, SLABS, rows, LANES), jnp.bfloat16),
            pltpu.VMEM((FFT_LO * chunk, 2 * FFT_HI), jnp.bfloat16),
            pltpu.SemaphoreType.DMA((5,)),
            pltpu.SemaphoreType.DMA((2 * groups,)),
            pltpu.SemaphoreType.DMA((n_tm, groups)),
            pltpu.SemaphoreType.DMA((n_fq, span, groups)),
            pltpu.SemaphoreType.DMA((2,)),
            pltpu.SemaphoreType.DMA((2,)),
        ],
        compiler_params=pltpu.CompilerParams(
            collective_id=0, has_side_effects=True, vmem_limit_bytes=54 * 1024 * 1024
        ),
        name="grid_exchange_transform",
    )(
        strengths,
        sample_cell.reshape(samples // LANES, LANES),
        sample_frac.reshape(samples // LANES, LANES),
        jnp.asarray(np.cos(low), jnp.float32),
        jnp.asarray(np.sin(low), jnp.float32),
        jnp.asarray(full.astype(jnp.bfloat16)),
    )
    return pl.pallas_call(
        write_kernel,
        out_shape=jax.ShapeDtypeStruct(y_shape, jnp.float32),
        in_specs=[vmem],
        out_specs=pl.BlockSpec(memory_space=pl.ANY),
        scratch_shapes=[pltpu.SemaphoreType.DMA((parts * n_fq * groups,))],
        compiler_params=pltpu.CompilerParams(vmem_limit_bytes=16 * 1024 * 1024),
        name="write_out",
    )(y)


def solution(mesh):
    placed = (P(None, "freq", None, "tm"), P("tm"), P("tm"))
    return jax.shard_map(
        shards,
        mesh=mesh,
        in_specs=placed,
        out_specs=P(None, None, "tm", "freq", None, None),
        check_vma=False,
    )
```

time: 127 us -> 105 us (0.83)
  Pallas kernels: 119 us -> 105 us
  local copies, waits for them, and re-layouts: 7.11 us -> 0 us
    pallas_call x1, Pallas kernels: 116 us -> 101 us  [shards(): pl.pallas_call(functools.partial(main_kernel, n_tm, n_fq), out_shape=pltp...]
    unnamed x12 -> x0, local copies, waits for them, and re-layouts: 7.11 us -> none
where the time goes in v2:
time: 105 us
  Pallas kernels  105 us (100%)
    pallas_call x1, Pallas kernels, shards(): pl.pallas_call(functools.partial(main_kernel, n_tm, n_fq), out_shape=pltp...  101 us
    pallas_call x1, Pallas kernels, shards(): pl.pallas_call(write_kernel, out_shape=jax.ShapeDtypeStruct(y_shape, jnp....  3.42 us

profile of v2, /device:TPU:5, one launch (start us, length us, event | category | flops | bytes accessed | tf_op | source)
XLA Modules:
  0.0 104.8 jit_solution(4327594447641945658)
XLA Ops:
  0.0 101.4 %grid_exchange_transform.1.y = f32[2,8,16,2,32,128]{5,4,3,2,1,0:T(8,128)S(1)} custom-call(bf16[2,4,256,2048]{3,2,1,0:T(8,128)(2,1)} %strengths.1, s32[16,128]{1,0:T(8,128)} %bitcast.2, f32[16,128]{1,0:T(8,128)} %bitcast.3, f32[32,128]{1,0:T(8,128)} %constant.6.clone.tc_hbm, f32[32,128]{1,0:T(8,128)} %constant.7.clone.ts_hbm, ...), custom_call_target="tpu_custom_call" | custom-call | tf_op jit(solution)/shard_map/grid_exchange_transform/pallas_call | solution.py:442
  101.4 3.4 %write_out.1 = f32[2,8,16,2,32,128]{5,4,3,2,1,0:T(8,128)} custom-call(f32[2,8,16,2,32,128]{5,4,3,2,1,0:T(8,128)S(1)} %grid_exchange_transform.1.y), custom_call_target="tpu_custom_call" | custom-call | tf_op jit(solution)/shard_map/write_out/pallas_call | solution.py:481

commit v3 on v2

--- a/solution.py
+++ b/solution.py
@@ -58,9 +58,30 @@
     return [int(format(i, "0%db" % bits)[::-1], 2) if bits else 0 for i in range(count)]
 
 
+def transform(blocks, m, g, chunk, tc, ts, hi, lhs, out, start, stride):
+    re, im = [], []
+    for n in range(FFT_LO):
+        tile = blocks[m * PER_FRAME + n // SLABS, g, PLACE[n % SLABS]]
+        re.append(tile[:chunk].astype(jnp.float32))
+        im.append(tile[chunk:].astype(jnp.float32))
+    re, im = fft_list(re, im)
+    for a in range(FFT_LO):
+        cc = tc[a : a + 1, :]
+        ss = ts[a : a + 1, :]
+        at = pl.ds(a * chunk, chunk)
+        lhs[at, :FFT_HI] = (re[a] * cc + im[a] * ss).astype(jnp.bfloat16)
+        lhs[at, FFT_HI:] = (im[a] * cc - re[a] * ss).astype(jnp.bfloat16)
+    y = jnp.dot(lhs[...], hi[...], preferred_element_type=jnp.float32)
+    for a in range(FFT_LO):
+        for p in range(2):
+            out[p, pl.ds(start + a, chunk, stride=stride), :] = y[
+                a * chunk : (a + 1) * chunk, p * FFT_HI : (p + 1) * FFT_HI
+            ]
+
+
 def main_kernel(
-    n_tm, n_fq, strengths, cell_hbm, frac_hbm, tc_hbm, ts_hbm, hi_hbm, y,
-    xv, cell, frac, tc, ts, hi, cols, fracs, table, edge_out, halo, src, recv, lhs,
+    n_tm, n_fq, strengths, cell_hbm, frac_hbm, tc_hbm, ts_hbm, hi_hbm, y, recv, tc, ts, hi,
+    xv, cell, frac, cols, fracs, table, edge_out, halo, src, lhs,
     small, load, send, arrive, halo_send, halo_arrive,
 ):
     t = lax.axis_index("tm")
@@ -199,7 +220,7 @@
         return pltpu.make_async_remote_copy(
             src_ref=src.at[(d,) + part],
             dst_ref=recv.at[(f, slot) + part],
-            send_sem=send.at[d, g],
+            send_sem=send.at[lax.div(d, half), g],
             recv_sem=arrive.at[f, slot, g],
             device_id=(d, home),
             device_id_type=MESH,
@@ -315,7 +336,7 @@
         return pltpu.make_async_remote_copy(
             src_ref=src.at[0, pl.ds(g, pair)],
             dst_ref=recv.at[source, s, pl.ds(g, pair)],
-            send_sem=send.at[0, g],
+            send_sem=send.at[0, 0],
             recv_sem=arrive.at[source, s, g],
             device_id=(t, f),
             device_id_type=MESH,
@@ -334,22 +355,61 @@
     ready = min(2, groups)
     turns = frames * groups
 
-    def sent(i, c):
-        d, g = lax.div(i, groups), lax.rem(i, groups)
-        away = (d != t) | (home != f)
-        two = paired(t, d)
-
-        @pl.when(away & jnp.logical_not(two))
+    def sent(side, g, count, pair=1):
+        part = src.at[pl.ds(side * half, count), pl.ds(g, pair)]
+        pltpu.make_async_remote_copy(
+            src_ref=part,
+            dst_ref=part,
+            send_sem=send.at[side, g],
+            recv_sem=arrive.at[0, 0, 0],
+            device_id=(right, f),
+            device_id_type=MESH,
+        ).wait_send()
+
+    def all_sent(g, c):
+        @pl.when(keep)
         def _():
-            copy_out(d, g, 0, SLABS).wait_send()
-
-        if both == 2:
-
-            @pl.when(away & two & (lax.rem(g, 2) == 0))
-            def _():
-                copy_out(d, g, 0, SLABS, both).wait_send()
-
-        return c
+            sent(upper, g, half - 1)
+
+        @pl.when(jnp.logical_not(keep))
+        def _():
+            sent(upper, g, half)
+
+        if both == 1:
+            sent(1 - upper, g, half)
+        else:
+
+            @pl.when(jnp.logical_not(outer))
+            def _():
+                sent(1 - upper, g, half)
+
+            @pl.when(outer & (lax.rem(g, 2) == 0))
+            def _():
+                sent(1 - upper, g, half, both)
+
+        return c
+
+    def await_unit(source, m, g):
+        def await_one(s, c):
+            slot_in = m * PER_FRAME + s
+            origin = f * span + slot_in
+            away = (source != f) | (origin != t)
+            two = paired(origin, t)
+
+            @pl.when(away & jnp.logical_not(two))
+            def _():
+                landed(source, slot_in, g).wait_recv()
+
+            if both == 2:
+
+                @pl.when(away & two & (lax.rem(g, 2) == 0))
+                def _():
+                    landed(source, slot_in, lax.div(g, both) * both, both).wait_recv()
+
+            return c
+
+        with jax.named_scope("await"):
+            lax.fori_loop(0, PER_FRAME, await_one, 0)
 
     def unit(i, c):
         n = lax.div(i, n_fq)
@@ -360,69 +420,70 @@
         inward = first | last
         g = jnp.where(first, n, jnp.where(last, late, lax.rem(n - ready, groups)))
         m = jnp.where(inward, 0, 1 + lax.div(n - ready, groups))
-        m = lax.rem(m + frames - 1 + f, frames)
-
-        def await_one(s, c):
-            slot_in = m * PER_FRAME + s
-            origin = f * span + slot_in
-            away = (source != f) | (origin != t)
-            two = paired(origin, t)
-
-            @pl.when(away & jnp.logical_not(two))
-            def _():
-                landed(source, slot_in, g).wait_recv()
-
-            if both == 2:
-
-                @pl.when(away & two & (lax.rem(g, 2) == 0))
-                def _():
-                    landed(source, slot_in, g, both).wait_recv()
-
-            return c
-
-        with jax.named_scope("await"):
-            lax.fori_loop(0, PER_FRAME, await_one, 0)
-        re, im = [], []
-        for n in range(FFT_LO):
-            tile = recv.at[source, m * PER_FRAME + n // SLABS, g, PLACE[n % SLABS]]
-            re.append(tile[:chunk].astype(jnp.float32))
-            im.append(tile[chunk:].astype(jnp.float32))
-        re, im = fft_list(re, im)
-        for a in range(FFT_LO):
-            cc = tc[a : a + 1, :]
-            ss = ts[a : a + 1, :]
-            at = pl.ds(a * chunk, chunk)
-            lhs[at, :FFT_HI] = (re[a] * cc + im[a] * ss).astype(jnp.bfloat16)
-            lhs[at, FFT_HI:] = (im[a] * cc - re[a] * ss).astype(jnp.bfloat16)
-        out = jnp.dot(lhs[...], hi[...], preferred_element_type=jnp.float32)
-        for a in range(FFT_LO):
-            for p in range(2):
-                flat[p, source * groups + g, pl.ds(m * FFT_LO + a, chunk, stride=frames * FFT_LO), :] = out[
-                    a * chunk : (a + 1) * chunk, p * FFT_HI : (p + 1) * FFT_HI
-                ]
-        return c
-
-    lax.fori_loop(0, turns * n_fq, unit, 0)
+        m = lax.rem(m + inner_frame(f, frames), frames)
+
+        await_unit(source, m, g)
+        transform(
+            recv.at[source], m, g, chunk, tc, ts, hi, lhs,
+            flat.at[:, source * groups + g], m * FFT_LO, frames * FFT_LO,
+        )
+        return c
+
+    lax.fori_loop(0, (turns - 1) * n_fq, unit, 0)
+
+    def await_last(i, c):
+        await_unit(lax.rem(f + i, n_fq), inner_frame(f, frames), groups - 1)
+        return c
+
+    lax.fori_loop(0, n_fq, await_last, 0)
     with jax.named_scope("sent"):
-        lax.fori_loop(0, n_tm * groups, sent, 0)
+        lax.fori_loop(0, groups, all_sent, 0)
         halo_copy(0, right).wait_send()
         halo_copy(1, left).wait_send()
 
 
-def write_kernel(y, out, sems):
-    parts, blocks = y.shape[0], y.shape[1]
-
-    def copies():
-        return [
-            pltpu.make_async_copy(y.at[p, b], out.at[p, b], sems.at[p * blocks + b])
-            for p in range(parts)
-            for b in range(blocks)
-        ]
-
-    for c in copies():
+def inner_frame(f, frames):
+    return lax.rem(frames - 1 + f, frames)
+
+
+def last_kernel(n_fq, y, recv, tc, ts, hi, out, tail, lhs, sems, tail_sems):
+    f = lax.axis_index("freq")
+    parts, blocks, chunk, frames = y.shape[:4]
+    groups = blocks // n_fq
+    mine = inner_frame(f, frames)
+    copies = []
+    for p in range(parts):
+        for b in range(blocks):
+            if b % groups < groups - 1:
+                copies.append((y.at[p, b], out.at[p, b]))
+            else:
+                for j in range(1, frames):
+                    m = lax.rem(mine + j, frames)
+                    copies.append((y.at[p, b, :, m], out.at[p, b, :, m]))
+    copies = [pltpu.make_async_copy(a, b, sems.at[i]) for i, (a, b) in enumerate(copies)]
+    for c in copies:
         c.start()
-    for c in copies():
+
+    def tail_copy(p, source):
+        return pltpu.make_async_copy(
+            tail.at[source, p], out.at[p, source * groups + groups - 1, :, mine], tail_sems.at[p, source]
+        )
+
+    def unit(source, c):
+        flat = tail.reshape(n_fq, parts, chunk * FFT_LO, FFT_HI)
+        transform(
+            recv.at[source], mine, groups - 1, chunk, tc, ts, hi, lhs, flat.at[source], 0, FFT_LO
+        )
+        for p in range(parts):
+            tail_copy(p, source).start()
+        return c
+
+    lax.fori_loop(0, n_fq, unit, 0)
+    for c in copies:
         c.wait()
+    for source in range(n_fq):
+        for p in range(parts):
+            tail_copy(p, source).wait()
 
 
 def shards(strengths, sample_cell, sample_frac):
@@ -439,35 +500,37 @@
     full = np.block([[hc, -hs], [hs, hc]]).astype(np.float32) / math.sqrt(FFTLEN)
     vmem = pl.BlockSpec(memory_space=pltpu.VMEM)
     y_shape = (parts, n_fq * groups, chunk, frames, FFT_LO, FFT_HI)
-    y = pl.pallas_call(
+    results = pl.pallas_call(
         functools.partial(main_kernel, n_tm, n_fq),
-        out_shape=pltpu.VMEM(y_shape, jnp.float32),
+        out_shape=(
+            pltpu.VMEM(y_shape, jnp.float32),
+            pltpu.VMEM((n_fq, span, groups, SLABS, rows, LANES), jnp.bfloat16),
+            pltpu.VMEM((FFT_LO, FFT_HI), jnp.float32),
+            pltpu.VMEM((FFT_LO, FFT_HI), jnp.float32),
+            pltpu.VMEM((2 * FFT_HI, 2 * FFT_HI), jnp.bfloat16),
+        ),
         in_specs=[pl.BlockSpec(memory_space=pltpu.HBM)] * 6,
-        out_specs=vmem,
+        out_specs=(vmem,) * 5,
         scratch_shapes=[
             pltpu.VMEM((parts, groups, channels, samples), jnp.bfloat16),
             pltpu.VMEM((samples // LANES, LANES), jnp.int32),
             pltpu.VMEM((samples // LANES, LANES), jnp.float32),
-            pltpu.VMEM((FFT_LO, FFT_HI), jnp.float32),
-            pltpu.VMEM((FFT_LO, FFT_HI), jnp.float32),
-            pltpu.VMEM((2 * FFT_HI, 2 * FFT_HI), jnp.bfloat16),
             pltpu.VMEM((samples, LANES), jnp.float32),
             pltpu.VMEM((samples, LANES), jnp.float32),
             pltpu.VMEM((samples, (SLABS + 1) * LANES), jnp.bfloat16),
             pltpu.VMEM((16, total), jnp.float32),
             pltpu.VMEM((LANES, total), jnp.float32),
             pltpu.VMEM((n_tm, groups, SLABS, rows, LANES), jnp.bfloat16),
-            pltpu.VMEM((n_fq, span, groups, SLABS, rows, LANES), jnp.bfloat16),
             pltpu.VMEM((FFT_LO * chunk, 2 * FFT_HI), jnp.bfloat16),
             pltpu.SemaphoreType.DMA((5,)),
             pltpu.SemaphoreType.DMA((2 * groups,)),
-            pltpu.SemaphoreType.DMA((n_tm, groups)),
+            pltpu.SemaphoreType.DMA((2, groups)),
             pltpu.SemaphoreType.DMA((n_fq, span, groups)),
             pltpu.SemaphoreType.DMA((2,)),
             pltpu.SemaphoreType.DMA((2,)),
         ],
         compiler_params=pltpu.CompilerParams(
-            collective_id=0, has_side_effects=True, vmem_limit_bytes=54 * 1024 * 1024
+            collective_id=0, has_side_effects=True, vmem_limit_bytes=48 * 1024 * 1024
         ),
         name="grid_exchange_transform",
     )(
@@ -479,14 +542,19 @@
         jnp.asarray(full.astype(jnp.bfloat16)),
     )
     return pl.pallas_call(
-        write_kernel,
+        functools.partial(last_kernel, n_fq),
         out_shape=jax.ShapeDtypeStruct(y_shape, jnp.float32),
-        in_specs=[vmem],
+        in_specs=[vmem] * 5,
         out_specs=pl.BlockSpec(memory_space=pl.ANY),
-        scratch_shapes=[pltpu.SemaphoreType.DMA((parts * n_fq * groups,))],
+        scratch_shapes=[
+            pltpu.VMEM((n_fq, parts, chunk, FFT_LO, FFT_HI), jnp.float32),
+            pltpu.VMEM((FFT_LO * chunk, 2 * FFT_HI), jnp.bfloat16),
+            pltpu.SemaphoreType.DMA((parts * n_fq * groups * frames,)),
+            pltpu.SemaphoreType.DMA((parts, n_fq)),
+        ],
         compiler_params=pltpu.CompilerParams(vmem_limit_bytes=16 * 1024 * 1024),
-        name="write_out",
-    )(y)
+        name="last_units_write",
+    )(*results)
 
 
 def solution(mesh):

time: 105 us -> 103 us (0.981)
  Pallas kernels: 105 us -> 103 us
    pallas_call x2, Pallas kernels: 105 us -> 103 us  [the longest x1 99.1 us: shards(): pl.pallas_call(functools.partial(main_kernel, n_tm, n_fq), out_shape=(plt...]
where the time goes in v3:
time: 103 us
  Pallas kernels  103 us (100%)
    pallas_call x1, Pallas kernels, shards(): pl.pallas_call(functools.partial(main_kernel, n_tm, n_fq), out_shape=(plt...  99.1 us
    pallas_call x1, Pallas kernels, shards(): pl.pallas_call(functools.partial(last_kernel, n_fq), out_shape=jax.ShapeD...  3.58 us

profile of v3, /device:TPU:5, one launch (start us, length us, event | category | flops | bytes accessed | tf_op | source)
XLA Modules:
  0.0 102.7 jit_solution(6361169474519043124)
XLA Ops:
  0.0 99.1 %grid_exchange_transform.1 = (f32[2,8,16,2,32,128]{5,4,3,2,1,0:T(8,128)S(1)}, bf16[2,8,4,8,32,128]{5,4,3,2,1,0:T(8,128)(2,1)S(1)}, f32[32,128]{1,0:T(8,128)S(1)}...) custom-call(bf16[2,4,256,2048]{3,2,1,0:T(8,128)(2,1)} %strengths.1, s32[16,128]{1,0:T(8,128)} %bitcast.2, f32[16,128]{1,0:T(8,128)} %bitcast.3, ...), custom_call_target="tpu_custom_call" | custom-call | tf_op jit(solution)/shard_map/grid_exchange_transform/pallas_call | solution.py:503
  99.1 3.6 %last_units_write.1 = f32[2,8,16,2,32,128]{5,4,3,2,1,0:T(8,128)} custom-call(f32[2,8,16,2,32,128]{5,4,3,2,1,0:T(8,128)S(1)} %get-tuple-element.10.y, bf16[2,8,4,8,32,128]{5,4,3,2,1,0:T(8,128)(2,1)S(1)} %get-tuple-element.11.recv, f32[32,128]{1,0:T(8,128)S(1)} %get-tuple-element.12.tc, f32[32,128]{1,0:T(8,128)S(1)} %get-tuple-element.13.ts, ...), custom_call_target="tpu_custom_call" | custom-call | tf_op jit(solution)/shard_map/last_units_write/pallas_call | solution.py:544

commit v4 on v3

--- a/solution.py
+++ b/solution.py
@@ -51,11 +51,8 @@
     return out_r, out_i
 
 
-def spread_order(count):
-    bits = count.bit_length() - 1
-    if 1 << bits != count:
-        return list(range(count))
-    return [int(format(i, "0%db" % bits)[::-1], 2) if bits else 0 for i in range(count)]
+def sequence(pairs):
+    return [(far, pair, core) for pair in reversed(range(pairs)) for core in range(2) for far in (1, 0)]
 
 
 def transform(blocks, m, g, chunk, tc, ts, hi, lhs, out, start, stride):
@@ -122,6 +119,27 @@
     for i in range(2):
         constants[i].start()
 
+    barrier = pltpu.get_barrier_semaphore()
+
+    def greet(i, c):
+        origin = f * span + lax.rem(slot + 1 + i, span)
+
+        def one(j, c):
+            other = lax.rem(f + j, n_fq)
+
+            @pl.when((origin != t) | (other != f))
+            def _():
+                pl.semaphore_signal(barrier, inc=1, device_id=(origin, other), device_id_type=MESH)
+
+            return c
+
+        return lax.fori_loop(0, n_fq, one, c)
+
+    with jax.named_scope("greet"):
+        lax.fori_loop(0, span, greet, 0)
+        for peer in (left, right):
+            pl.semaphore_signal(barrier, inc=1, device_id=(peer, f), device_id_type=MESH)
+
     def fetch(k):
         side, g = order(k)
         at = (slice(None), g, pl.ds(pl.multiple_of(side * wide, wide), wide))
@@ -129,32 +147,14 @@
 
     fetch(0).start()
 
-    barrier = pltpu.get_barrier_semaphore()
-
-    def greet(i, c):
-        origin = f * span + lax.rem(slot + 1 + i, span)
-
-        def one(j, c):
-            other = lax.rem(f + j, n_fq)
-
-            @pl.when((origin != t) | (other != f))
-            def _():
-                pl.semaphore_signal(barrier, inc=1, device_id=(origin, other), device_id_type=MESH)
-
-            return c
-
-        return lax.fori_loop(0, n_fq, one, c)
-
-    lax.fori_loop(0, span, greet, 0)
-    for peer in (left, right):
-        pl.semaphore_signal(barrier, inc=1, device_id=(peer, f), device_id_type=MESH)
-
-    for k in range(1, steps):
-        fetch(k).start()
+    with jax.named_scope('fetch'):
+        for k in range(1, steps):
+            fetch(k).start()
 
     base = t * GRID_DEV
-    constants[0].wait()
-    constants[1].wait()
+    with jax.named_scope('cw'):
+        constants[0].wait()
+        constants[1].wait()
     for i in range(samples // LANES):
         at = pl.ds(i * LANES, LANES)
         local = (cell[i : i + 1, :] - base).astype(jnp.float32)
@@ -203,9 +203,13 @@
 
     def with_halo(k, low, high):
         side, g = order(k)
+        at = pl.ds(pl.multiple_of(g * channels + side * wide, LANES), wide)
+        empty = jnp.zeros((LANES - 2 * HALF, wide), jnp.float32)
         outside = jnp.concatenate(
             [
-                halo[:, pl.ds(pl.multiple_of(g * 2 * block + p * channels + side * wide, LANES), wide)].T
+                jnp.concatenate(
+                    [halo[0, p * HALF : (p + 1) * HALF, at], empty, halo[1, p * HALF : (p + 1) * HALF, at]]
+                ).T
                 for p in range(parts)
             ]
         )
@@ -226,12 +230,19 @@
             device_id_type=MESH,
         )
 
-    spread = spread_order(half)
+    pairs = n_tm // 8
+    pair_at = lax.rem(lax.div(t, 2), pairs)
+    core_at = lax.rem(t, 2)
+
+    def target(side, far, pair, core):
+        across = lax.rem(side + 1 + far, 2)
+        return side * half + across * (half // 2) + lax.rem(pair_at + pair, pairs) * 2 + lax.rem(core_at + core, 2)
+
 
     def send_step(k, first, count, pair=1):
         side, g = order(k)
-        for i in range(half):
-            d = side * half + lax.rem(t + spread[i], half)
+        for far, pair_by, core_by in sequence(pairs):
+            d = target(side, far, pair_by, core_by)
 
             @pl.when((d != t) | (home != f))
             def _():
@@ -244,14 +255,15 @@
                 build(j, slab_columns(1 + j))
             put(0, first, slabs(product(0, first, count)))
             if first == 0:
-                pl.semaphore_wait(barrier, jnp.where(keep, n_tm + 1, n_tm + 2))
+                with jax.named_scope('bar'):
+                    pl.semaphore_wait(barrier, jnp.where(keep, n_tm + 1, n_tm + 2))
             send_step(0, first, count)
             if first == 0:
                 for i in range(2, 5):
                     constants[i].start()
 
     beyond = jnp.where(
-        lane < HALF, lane + GRID_DEV, jnp.where((lane >= 16 - HALF) & (lane < 16), lane - 16, -GRID_DEV)
+        lane < HALF, lane + GRID_DEV, jnp.where(lane < 2 * HALF, lane - 2 * HALF, -GRID_DEV)
     ).astype(jnp.float32)
 
     def edges(g, c):
@@ -260,7 +272,15 @@
             table[:, SLABS * LANES :],
             preferred_element_type=jnp.float32,
         )
-        edge_out[:, pl.ds(pl.multiple_of(g * 2 * block, LANES), 2 * block)] = acc.T[:16]
+        across = acc.T[: 2 * HALF]
+        at = pl.ds(pl.multiple_of(g * channels, LANES), channels)
+        for side in range(2):
+            edge_out[side, :, at] = jnp.concatenate(
+                [
+                    across[side * HALF : (side + 1) * HALF, p * channels : (p + 1) * channels]
+                    for p in range(parts)
+                ]
+            )
         return c
 
     with jax.named_scope("edges"):
@@ -268,12 +288,11 @@
         for k in range(1, steps):
             fetch(k).wait()
         lax.fori_loop(0, groups, edges, 0)
-        halo[8 : LANES - 8, :] = jnp.zeros((LANES - 16, halo.shape[1]), jnp.float32)
 
     def halo_copy(i, peer):
         return pltpu.make_async_remote_copy(
-            src_ref=edge_out.at[8 * i : 8 * i + 8],
-            dst_ref=halo.at[pl.ds(i * (LANES - 8), 8)],
+            src_ref=edge_out.at[i],
+            dst_ref=halo.at[i],
             send_sem=halo_send.at[i],
             recv_sem=halo_arrive.at[i],
             device_id=(peer, f),
@@ -518,8 +537,8 @@
             pltpu.VMEM((samples, LANES), jnp.float32),
             pltpu.VMEM((samples, LANES), jnp.float32),
             pltpu.VMEM((samples, (SLABS + 1) * LANES), jnp.bfloat16),
-            pltpu.VMEM((16, total), jnp.float32),
-            pltpu.VMEM((LANES, total), jnp.float32),
+            pltpu.VMEM((2, parts * HALF, total // parts), jnp.float32),
+            pltpu.VMEM((2, parts * HALF, total // parts), jnp.float32),
             pltpu.VMEM((n_tm, groups, SLABS, rows, LANES), jnp.bfloat16),
             pltpu.VMEM((FFT_LO * chunk, 2 * FFT_HI), jnp.bfloat16),
             pltpu.SemaphoreType.DMA((5,)),

time: 103 us -> 101 us (0.981)
  Pallas kernels: 103 us -> 101 us
    pallas_call x1, Pallas kernels: 99.1 us -> 97.5 us  [shards(): pl.pallas_call(functools.partial(main_kernel, n_tm, n_fq), out_shape=(plt...]
where the time goes in v4:
time: 101 us
  Pallas kernels  101 us (100%)
    pallas_call x1, Pallas kernels, shards(): pl.pallas_call(functools.partial(main_kernel, n_tm, n_fq), out_shape=(plt...  97.5 us
    pallas_call x1, Pallas kernels, shards(): pl.pallas_call(functools.partial(last_kernel, n_fq), out_shape=jax.ShapeD...  3.58 us

profile of v4, /device:TPU:5, one launch (start us, length us, event | category | flops | bytes accessed | tf_op | source)
XLA Modules:
  0.0 101.1 jit_solution(11484768877825807384)
XLA Ops:
  0.0 97.5 %grid_exchange_transform.1 = (f32[2,8,16,2,32,128]{5,4,3,2,1,0:T(8,128)S(1)}, bf16[2,8,4,8,32,128]{5,4,3,2,1,0:T(8,128)(2,1)S(1)}, f32[32,128]{1,0:T(8,128)S(1)}...) custom-call(bf16[2,4,256,2048]{3,2,1,0:T(8,128)(2,1)} %strengths.1, s32[16,128]{1,0:T(8,128)} %bitcast.2, f32[16,128]{1,0:T(8,128)} %bitcast.3, ...), custom_call_target="tpu_custom_call" | custom-call | tf_op jit(solution)/shard_map/grid_exchange_transform/pallas_call | solution.py:522
  97.5 3.6 %last_units_write.1 = f32[2,8,16,2,32,128]{5,4,3,2,1,0:T(8,128)} custom-call(f32[2,8,16,2,32,128]{5,4,3,2,1,0:T(8,128)S(1)} %get-tuple-element.10.y, bf16[2,8,4,8,32,128]{5,4,3,2,1,0:T(8,128)(2,1)S(1)} %get-tuple-element.11.recv, f32[32,128]{1,0:T(8,128)S(1)} %get-tuple-element.12.tc, f32[32,128]{1,0:T(8,128)S(1)} %get-tuple-element.13.ts, ...), custom_call_target="tpu_custom_call" | custom-call | tf_op jit(solution)/shard_map/last_units_write/pallas_call | solution.py:563

commit v5 on v4

--- a/solution.py
+++ b/solution.py
@@ -22,7 +22,7 @@
 INNER = SLABS - 2
 PER_FRAME = FFTLEN // GRID_DEV
 EARLY = 3
-FIRST = ((0, 2), (2, 4))
+FIRST = ((0, 2), (2, 2), (4, 2))
 PLACE = [INNER] + list(range(INNER)) + [INNER + 1]
 
 
@@ -79,7 +79,7 @@
 def main_kernel(
     n_tm, n_fq, strengths, cell_hbm, frac_hbm, tc_hbm, ts_hbm, hi_hbm, y, recv, tc, ts, hi,
     xv, cell, frac, cols, fracs, table, edge_out, halo, src, lhs,
-    small, load, send, arrive, halo_send, halo_arrive,
+    small, load, send, arrive, halo_send, halo_arrive, ready,
 ):
     t = lax.axis_index("tm")
     f = lax.axis_index("freq")
@@ -87,7 +87,7 @@
     chunk = channels // n_tm
     rows = src.shape[3]
     wide = channels // 2
-    both = 2 if groups % 2 == 0 else 1
+    both = groups
     span = n_tm // n_fq
     frames = span // PER_FRAME
     slot = lax.rem(t, span)
@@ -120,25 +120,52 @@
         constants[i].start()
 
     barrier = pltpu.get_barrier_semaphore()
+    size = n_tm // 4
+    mate = jnp.where((quarter == 0) | (quarter == 2), t + size, t - size)
+
+    def outer_of(index):
+        q = lax.div(index, size)
+        return jnp.where(q == 1, index - size, jnp.where(q == 2, index + size, index))
+
+    def greet_one(tm, freq):
+        pl.semaphore_signal(barrier, inc=1, device_id=(tm, freq), device_id_type=MESH)
 
     def greet(i, c):
         origin = f * span + lax.rem(slot + 1 + i, span)
+        host = outer_of(origin)
+        facing = jnp.logical_not(outer) & (lax.div(origin, size) == 3 - quarter)
 
         def one(j, c):
             other = lax.rem(f + j, n_fq)
 
-            @pl.when((origin != t) | (other != f))
-            def _():
-                pl.semaphore_signal(barrier, inc=1, device_id=(origin, other), device_id_type=MESH)
+            @pl.when(facing)
+            def _():
+                greet_one(origin, other)
+
+            @pl.when((host != t) | (other != f))
+            def _():
+                greet_one(host, other)
 
             return c
 
         return lax.fori_loop(0, n_fq, one, c)
 
-    with jax.named_scope("greet"):
-        lax.fori_loop(0, span, greet, 0)
-        for peer in (left, right):
-            pl.semaphore_signal(barrier, inc=1, device_id=(peer, f), device_id_type=MESH)
+    lax.fori_loop(0, span, greet, 0)
+    greet_one(outer_of(left), f)
+    greet_one(outer_of(right), f)
+
+    @pl.when(jnp.logical_not(outer))
+    def _():
+        greet_one(mate, f)
+
+    def greeted():
+        own = jnp.where(keep, n_tm - 1, n_tm)
+        others = jnp.where(lax.div(mate, span) == f, n_tm - 1, n_tm)
+        pl.semaphore_wait(barrier, jnp.where(outer, own + others + 5, size))
+
+        @pl.when(outer)
+        def _():
+            pl.semaphore_signal(ready, inc=1, device_id=(mate, f), device_id_type=MESH)
 
     def fetch(k):
         side, g = order(k)
@@ -147,14 +174,12 @@
 
     fetch(0).start()
 
-    with jax.named_scope('fetch'):
-        for k in range(1, steps):
-            fetch(k).start()
+    for k in range(1, steps):
+        fetch(k).start()
 
     base = t * GRID_DEV
-    with jax.named_scope('cw'):
-        constants[0].wait()
-        constants[1].wait()
+    constants[0].wait()
+    constants[1].wait()
     for i in range(samples // LANES):
         at = pl.ds(i * LANES, LANES)
         local = (cell[i : i + 1, :] - base).astype(jnp.float32)
@@ -239,9 +264,11 @@
         return side * half + across * (half // 2) + lax.rem(pair_at + pair, pairs) * 2 + lax.rem(core_at + core, 2)
 
 
-    def send_step(k, first, count, pair=1):
+    def send_step(k, first, count, pair=1, which=(0, 1)):
         side, g = order(k)
         for far, pair_by, core_by in sequence(pairs):
+            if far not in which:
+                continue
             d = target(side, far, pair_by, core_by)
 
             @pl.when((d != t) | (home != f))
@@ -255,12 +282,20 @@
                 build(j, slab_columns(1 + j))
             put(0, first, slabs(product(0, first, count)))
             if first == 0:
-                with jax.named_scope('bar'):
-                    pl.semaphore_wait(barrier, jnp.where(keep, n_tm + 1, n_tm + 2))
-            send_step(0, first, count)
+                with jax.named_scope("bar"):
+                    greeted()
+            send_step(0, first, count, which=(0,))
             if first == 0:
                 for i in range(2, 5):
                     constants[i].start()
+
+        with jax.named_scope("ready"):
+
+            @pl.when(jnp.logical_not(outer))
+            def _():
+                pl.semaphore_wait(ready, 1)
+
+        send_step(0, 0, INNER, which=(1,))
 
     beyond = jnp.where(
         lane < HALF, lane + GRID_DEV, jnp.where(lane < 2 * HALF, lane - 2 * HALF, -GRID_DEV)
@@ -328,7 +363,7 @@
         else:
             in_pairs = outer & (k >= groups)
 
-            @pl.when(in_pairs & (lax.rem(k, 2) == 1))
+            @pl.when(in_pairs & (lax.rem(k, both) == both - 1))
             def _():
                 send_step(k, 0, SLABS, both)
 
@@ -366,7 +401,7 @@
         return (q == 0) | (q == 3)
 
     def paired(origin, d):
-        return is_outer(origin) & (lax.div(origin, half) != lax.div(d, half)) & (both == 2)
+        return is_outer(origin) & (lax.div(origin, half) != lax.div(d, half)) & (both > 1)
 
     for i in range(2, 5):
         constants[i].wait()
@@ -402,7 +437,7 @@
             def _():
                 sent(1 - upper, g, half)
 
-            @pl.when(outer & (lax.rem(g, 2) == 0))
+            @pl.when(outer & (lax.rem(g, both) == 0))
             def _():
                 sent(1 - upper, g, half, both)
 
@@ -419,9 +454,9 @@
             def _():
                 landed(source, slot_in, g).wait_recv()
 
-            if both == 2:
-
-                @pl.when(away & two & (lax.rem(g, 2) == 0))
+            if both > 1:
+
+                @pl.when(away & two & (lax.rem(g, both) == 0))
                 def _():
                     landed(source, slot_in, lax.div(g, both) * both, both).wait_recv()
 
@@ -547,6 +582,7 @@
             pltpu.SemaphoreType.DMA((n_fq, span, groups)),
             pltpu.SemaphoreType.DMA((2,)),
             pltpu.SemaphoreType.DMA((2,)),
+            pltpu.SemaphoreType.REGULAR,
         ],
         compiler_params=pltpu.CompilerParams(
             collective_id=0, has_side_effects=True, vmem_limit_bytes=48 * 1024 * 1024

time: 101 us -> 101 us (level)
  no operation moved by 1% of the time
where the time goes in v5:
time: 101 us
  Pallas kernels  101 us (100%)
    pallas_call x1, Pallas kernels, shards(): pl.pallas_call(functools.partial(main_kernel, n_tm, n_fq), out_shape=(plt...  97 us
    pallas_call x1, Pallas kernels, shards(): pl.pallas_call(functools.partial(last_kernel, n_fq), out_shape=jax.ShapeD...  3.58 us

profile of v5, /device:TPU:5, one launch (start us, length us, event | category | flops | bytes accessed | tf_op | source)
XLA Modules:
  0.0 100.6 jit_solution(5609598532005982420)
XLA Ops:
  0.0 97.0 %grid_exchange_transform.1 = (f32[2,8,16,2,32,128]{5,4,3,2,1,0:T(8,128)S(1)}, bf16[2,8,4,8,32,128]{5,4,3,2,1,0:T(8,128)(2,1)S(1)}, f32[32,128]{1,0:T(8,128)S(1)}...) custom-call(bf16[2,4,256,2048]{3,2,1,0:T(8,128)(2,1)} %strengths.1, s32[16,128]{1,0:T(8,128)} %bitcast.2, f32[16,128]{1,0:T(8,128)} %bitcast.3, ...), custom_call_target="tpu_custom_call" | custom-call | tf_op jit(solution)/shard_map/grid_exchange_transform/pallas_call | solution.py:557
  97.0 3.6 %last_units_write.1 = f32[2,8,16,2,32,128]{5,4,3,2,1,0:T(8,128)} custom-call(f32[2,8,16,2,32,128]{5,4,3,2,1,0:T(8,128)S(1)} %get-tuple-element.10.y, bf16[2,8,4,8,32,128]{5,4,3,2,1,0:T(8,128)(2,1)S(1)} %get-tuple-element.11.recv, f32[32,128]{1,0:T(8,128)S(1)} %get-tuple-element.12.tc, f32[32,128]{1,0:T(8,128)S(1)} %get-tuple-element.13.ts, ...), custom_call_target="tpu_custom_call" | custom-call | tf_op jit(solution)/shard_map/last_units_write/pallas_call | solution.py:599

commit v6 on v5

--- a/solution.py
+++ b/solution.py
@@ -167,15 +167,20 @@
         def _():
             pl.semaphore_signal(ready, inc=1, device_id=(mate, f), device_id_type=MESH)
 
-    def fetch(k):
-        side, g = order(k)
-        at = (slice(None), g, pl.ds(pl.multiple_of(side * wide, wide), wide))
-        return pltpu.make_async_copy(strengths.at[at], xv.at[at], load.at[k])
-
+    def fetch(i):
+        if i == 2:
+            at = (slice(None), pl.ds(1, groups - 1))
+        else:
+            side = order(0)[0]
+            side = side if i == 0 else 1 - side
+            at = (slice(None), 0, pl.ds(pl.multiple_of(side * wide, wide), wide))
+        return pltpu.make_async_copy(strengths.at[at], xv.at[at], load.at[i])
+
+    fetches = 3 if groups > 1 else 2
     fetch(0).start()
 
-    for k in range(1, steps):
-        fetch(k).start()
+    for i in range(1, fetches):
+        fetch(i).start()
 
     base = t * GRID_DEV
     constants[0].wait()
@@ -249,8 +254,8 @@
         return pltpu.make_async_remote_copy(
             src_ref=src.at[(d,) + part],
             dst_ref=recv.at[(f, slot) + part],
-            send_sem=send.at[lax.div(d, half), g],
-            recv_sem=arrive.at[f, slot, g],
+            send_sem=send.at[lax.div(d, half)],
+            recv_sem=arrive.at[f, lax.div(slot, PER_FRAME), g],
             device_id=(d, home),
             device_id_type=MESH,
         )
@@ -320,8 +325,8 @@
 
     with jax.named_scope("edges"):
         build(SLABS, beyond)
-        for k in range(1, steps):
-            fetch(k).wait()
+        for i in range(1, fetches):
+            fetch(i).wait()
         lax.fori_loop(0, groups, edges, 0)
 
     def halo_copy(i, peer):
@@ -386,12 +391,13 @@
 
         lax.fori_loop(0, groups, own, 0)
 
-    def landed(source, s, g, pair=1):
+    def landed(source, m, g, pair=1, count=PER_FRAME):
+        part = recv.at[source, pl.ds(m * PER_FRAME, count), pl.ds(g, pair)]
         return pltpu.make_async_remote_copy(
-            src_ref=src.at[0, pl.ds(g, pair)],
-            dst_ref=recv.at[source, s, pl.ds(g, pair)],
-            send_sem=send.at[0, 0],
-            recv_sem=arrive.at[source, s, g],
+            src_ref=part,
+            dst_ref=part,
+            send_sem=send.at[0],
+            recv_sem=arrive.at[source, m, g],
             device_id=(t, f),
             device_id_type=MESH,
         )
@@ -409,61 +415,47 @@
     ready = min(2, groups)
     turns = frames * groups
 
-    def sent(side, g, count, pair=1):
-        part = src.at[pl.ds(side * half, count), pl.ds(g, pair)]
+    def sent(side, count):
+        part = src.at[pl.ds(side * half, count)]
         pltpu.make_async_remote_copy(
             src_ref=part,
             dst_ref=part,
-            send_sem=send.at[side, g],
+            send_sem=send.at[side],
             recv_sem=arrive.at[0, 0, 0],
             device_id=(right, f),
             device_id_type=MESH,
         ).wait_send()
 
-    def all_sent(g, c):
+    def all_sent():
         @pl.when(keep)
         def _():
-            sent(upper, g, half - 1)
+            sent(upper, half - 1)
 
         @pl.when(jnp.logical_not(keep))
         def _():
-            sent(upper, g, half)
-
-        if both == 1:
-            sent(1 - upper, g, half)
-        else:
-
-            @pl.when(jnp.logical_not(outer))
-            def _():
-                sent(1 - upper, g, half)
-
-            @pl.when(outer & (lax.rem(g, both) == 0))
-            def _():
-                sent(1 - upper, g, half, both)
-
-        return c
+            sent(upper, half)
+
+        sent(1 - upper, half)
 
     def await_unit(source, m, g):
-        def await_one(s, c):
-            slot_in = m * PER_FRAME + s
-            origin = f * span + slot_in
-            away = (source != f) | (origin != t)
-            two = paired(origin, t)
-
-            @pl.when(away & jnp.logical_not(two))
-            def _():
-                landed(source, slot_in, g).wait_recv()
+        origin = f * span + m * PER_FRAME
+        own = (source == f) & (lax.div(t, PER_FRAME) == lax.div(origin, PER_FRAME))
+        two = paired(origin, t)
+        with jax.named_scope("await"):
+
+            @pl.when(own)
+            def _():
+                landed(source, m, g, count=PER_FRAME - 1).wait_recv()
+
+            @pl.when(jnp.logical_not(own | two))
+            def _():
+                landed(source, m, g).wait_recv()
 
             if both > 1:
 
-                @pl.when(away & two & (lax.rem(g, both) == 0))
+                @pl.when(two & (lax.rem(g, both) == 0))
                 def _():
-                    landed(source, slot_in, lax.div(g, both) * both, both).wait_recv()
-
-            return c
-
-        with jax.named_scope("await"):
-            lax.fori_loop(0, PER_FRAME, await_one, 0)
+                    landed(source, m, lax.div(g, both) * both, both).wait_recv()
 
     def unit(i, c):
         n = lax.div(i, n_fq)
@@ -491,7 +483,7 @@
 
     lax.fori_loop(0, n_fq, await_last, 0)
     with jax.named_scope("sent"):
-        lax.fori_loop(0, groups, all_sent, 0)
+        all_sent()
         halo_copy(0, right).wait_send()
         halo_copy(1, left).wait_send()
 
@@ -500,44 +492,40 @@
     return lax.rem(frames - 1 + f, frames)
 
 
-def last_kernel(n_fq, y, recv, tc, ts, hi, out, tail, lhs, sems, tail_sems):
+def last_kernel(n_fq, y, recv, tc, ts, hi, out, tail, lhs, sems):
     f = lax.axis_index("freq")
     parts, blocks, chunk, frames = y.shape[:4]
     groups = blocks // n_fq
     mine = inner_frame(f, frames)
-    copies = []
+    def copy(a, b, i):
+        return pltpu.make_async_copy(a, b, sems.at[i])
+
     for p in range(parts):
         for b in range(blocks):
             if b % groups < groups - 1:
-                copies.append((y.at[p, b], out.at[p, b]))
+                copy(y.at[p, b], out.at[p, b], 0).start()
             else:
                 for j in range(1, frames):
                     m = lax.rem(mine + j, frames)
-                    copies.append((y.at[p, b, :, m], out.at[p, b, :, m]))
-    copies = [pltpu.make_async_copy(a, b, sems.at[i]) for i, (a, b) in enumerate(copies)]
-    for c in copies:
-        c.start()
-
-    def tail_copy(p, source):
-        return pltpu.make_async_copy(
-            tail.at[source, p], out.at[p, source * groups + groups - 1, :, mine], tail_sems.at[p, source]
-        )
+                    copy(y.at[p, b, :, m], out.at[p, b, :, m], 1).start()
 
     def unit(source, c):
-        flat = tail.reshape(n_fq, parts, chunk * FFT_LO, FFT_HI)
+        flat = tail.reshape(parts, n_fq, chunk * FFT_LO, FFT_HI)
         transform(
-            recv.at[source], mine, groups - 1, chunk, tc, ts, hi, lhs, flat.at[source], 0, FFT_LO
+            recv.at[source], mine, groups - 1, chunk, tc, ts, hi, lhs, flat.at[:, source], 0, FFT_LO
         )
         for p in range(parts):
-            tail_copy(p, source).start()
+            copy(tail.at[p, source], out.at[p, source * groups + groups - 1, :, mine], 2).start()
         return c
 
     lax.fori_loop(0, n_fq, unit, 0)
-    for c in copies:
-        c.wait()
-    for source in range(n_fq):
-        for p in range(parts):
-            tail_copy(p, source).wait()
+    if groups > 1:
+        at = (slice(None), pl.ds(0, n_fq * (groups - 1)))
+        copy(y.at[at], out.at[at], 0).wait()
+    if frames > 1:
+        at = (slice(None), pl.ds(0, n_fq), slice(None), pl.ds(0, frames - 1))
+        copy(y.at[at], out.at[at], 1).wait()
+    copy(tail, out.at[:, pl.ds(0, n_fq), :, 0], 2).wait()
 
 
 def shards(strengths, sample_cell, sample_frac):
@@ -577,9 +565,9 @@
             pltpu.VMEM((n_tm, groups, SLABS, rows, LANES), jnp.bfloat16),
             pltpu.VMEM((FFT_LO * chunk, 2 * FFT_HI), jnp.bfloat16),
             pltpu.SemaphoreType.DMA((5,)),
-            pltpu.SemaphoreType.DMA((2 * groups,)),
-            pltpu.SemaphoreType.DMA((2, groups)),
-            pltpu.SemaphoreType.DMA((n_fq, span, groups)),
+            pltpu.SemaphoreType.DMA((3,)),
+            pltpu.SemaphoreType.DMA((2,)),
+            pltpu.SemaphoreType.DMA((n_fq, frames, groups)),
             pltpu.SemaphoreType.DMA((2,)),
             pltpu.SemaphoreType.DMA((2,)),
             pltpu.SemaphoreType.REGULAR,
@@ -602,10 +590,9 @@
         in_specs=[vmem] * 5,
         out_specs=pl.BlockSpec(memory_space=pl.ANY),
         scratch_shapes=[
-            pltpu.VMEM((n_fq, parts, chunk, FFT_LO, FFT_HI), jnp.float32),
+            pltpu.VMEM((parts, n_fq, chunk, FFT_LO, FFT_HI), jnp.float32),
             pltpu.VMEM((FFT_LO * chunk, 2 * FFT_HI), jnp.bfloat16),
-            pltpu.SemaphoreType.DMA((parts * n_fq * groups * frames,)),
-            pltpu.SemaphoreType.DMA((parts, n_fq)),
+            pltpu.SemaphoreType.DMA((3,)),
         ],
         compiler_params=pltpu.CompilerParams(vmem_limit_bytes=16 * 1024 * 1024),
         name="last_units_write",

time: 101 us -> 100 us (0.990)
  Pallas kernels: 101 us -> 99.7 us
where the time goes in v6:
time: 100 us; the launch traced here: 99.7 us
  Pallas kernels  99.7 us (100%)
    pallas_call x1, Pallas kernels, shards(): pl.pallas_call(functools.partial(main_kernel, n_tm, n_fq), out_shape=(plt...  96.4 us
    pallas_call x1, Pallas kernels, shards(): pl.pallas_call(functools.partial(last_kernel, n_fq), out_shape=jax.ShapeD...  3.29 us

profile of v6, /device:TPU:5, one launch (start us, length us, event | category | flops | bytes accessed | tf_op | source)
XLA Modules:
  0.0 99.7 jit_solution(17979626010988270938)
XLA Ops:
  0.0 96.4 %grid_exchange_transform.1 = (f32[2,8,16,2,32,128]{5,4,3,2,1,0:T(8,128)S(1)}, bf16[2,8,4,8,32,128]{5,4,3,2,1,0:T(8,128)(2,1)S(1)}, f32[32,128]{1,0:T(8,128)S(1)}...) custom-call(bf16[2,4,256,2048]{3,2,1,0:T(8,128)(2,1)} %strengths.1, s32[16,128]{1,0:T(8,128)} %bitcast.2, f32[16,128]{1,0:T(8,128)} %bitcast.3, ...), custom_call_target="tpu_custom_call" | custom-call | tf_op jit(solution)/shard_map/grid_exchange_transform/pallas_call | solution.py:545
  96.5 3.3 %last_units_write.1 = f32[2,8,16,2,32,128]{5,4,3,2,1,0:T(8,128)} custom-call(f32[2,8,16,2,32,128]{5,4,3,2,1,0:T(8,128)S(1)} %get-tuple-element.10.y, bf16[2,8,4,8,32,128]{5,4,3,2,1,0:T(8,128)(2,1)S(1)} %get-tuple-element.11.recv, f32[32,128]{1,0:T(8,128)S(1)} %get-tuple-element.12.tc, f32[32,128]{1,0:T(8,128)S(1)} %get-tuple-element.13.ts, ...), custom_call_target="tpu_custom_call" | custom-call | tf_op jit(solution)/shard_map/last_units_write/pallas_call | solution.py:587

commit v7 on v6

--- a/solution.py
+++ b/solution.py
@@ -21,7 +21,7 @@
 SLABS = GRID_DEV // LANES
 INNER = SLABS - 2
 PER_FRAME = FFTLEN // GRID_DEV
-EARLY = 3
+EARLY = 2
 FIRST = ((0, 2), (2, 2), (4, 2))
 PLACE = [INNER] + list(range(INNER)) + [INNER + 1]
 

time: 100 us -> 99.9 us (level)
  no operation moved by 1% of the time
where the time goes in v7:
time: 99.9 us; the launch traced here: 99.7 us
  Pallas kernels  99.7 us (100%)
    pallas_call x1, Pallas kernels, shards(): pl.pallas_call(functools.partial(main_kernel, n_tm, n_fq), out_shape=(plt...  96.4 us
    pallas_call x1, Pallas kernels, shards(): pl.pallas_call(functools.partial(last_kernel, n_fq), out_shape=jax.ShapeD...  3.29 us

profile of v7, /device:TPU:5, one launch (start us, length us, event | category | flops | bytes accessed | tf_op | source)
XLA Modules:
  0.0 99.7 jit_solution(6498811124495478855)
XLA Ops:
  0.0 96.4 %grid_exchange_transform.1 = (f32[2,8,16,2,32,128]{5,4,3,2,1,0:T(8,128)S(1)}, bf16[2,8,4,8,32,128]{5,4,3,2,1,0:T(8,128)(2,1)S(1)}, f32[32,128]{1,0:T(8,128)S(1)}...) custom-call(bf16[2,4,256,2048]{3,2,1,0:T(8,128)(2,1)} %strengths.1, s32[16,128]{1,0:T(8,128)} %bitcast.2, f32[16,128]{1,0:T(8,128)} %bitcast.3, ...), custom_call_target="tpu_custom_call" | custom-call | tf_op jit(solution)/shard_map/grid_exchange_transform/pallas_call | solution.py:545
  96.4 3.3 %last_units_write.1 = f32[2,8,16,2,32,128]{5,4,3,2,1,0:T(8,128)} custom-call(f32[2,8,16,2,32,128]{5,4,3,2,1,0:T(8,128)S(1)} %get-tuple-element.10.y, bf16[2,8,4,8,32,128]{5,4,3,2,1,0:T(8,128)(2,1)S(1)} %get-tuple-element.11.recv, f32[32,128]{1,0:T(8,128)S(1)} %get-tuple-element.12.tc, f32[32,128]{1,0:T(8,128)S(1)} %get-tuple-element.13.ts, ...), custom_call_target="tpu_custom_call" | custom-call | tf_op jit(solution)/shard_map/last_units_write/pallas_call | solution.py:587
